TPU v7x, 32 devices: a whole 2x2x4 slice. The times are simulated.
32 devices in a mesh: row: 8 (over y, x, core), col: 4 (over z).
Axes of the slice: x: 2, y: 2, z: 4, core: 2. Of those that a mesh axis runs over, the one named last changes fastest.
Arguments:
- slc_stack: float32 [20, 2, 64, 512], P(None, None, 'row', 'col'), may hold values from -6 to 6
- land_mask: int32 [64, 512], P('row', 'col'), may hold values from 0 to 1, as said below
Outputs:
- linked: float32 [20, 2, 64, 512], P(None, None, 'row', 'col')
- compressed_final: float32 [2, 64, 512], P(None, 'row', 'col')
- mean_strength: float32 [2], replicated
Inputs may be any that keep to these rules, and one draw needn't show every extreme that they name: `land_mask`: 1 marks a valid pixel, 0 a water pixel.
All inputs are finite; a program needn't handle non-finite values.
Results may differ from a plain program's by a relative error of at most 0.00012.
Values sent between devices are 32-bit elements; how exact they have to be, the bound alone decides.
A program may use at most 64 MiB of HBM per device.

v0:
```python
import functools

import jax
import jax.numpy as jnp
from jax import lax
from jax.experimental import pallas as pl
from jax.experimental.pallas import tpu as pltpu
from jax.sharding import PartitionSpec as P

M = 10
MS = 2
WIN = 11
ITERS = 4
REACH = WIN // 2
SUB = 8

covariance_floor = 8.0

AROUND = ((-1, 0), (1, 0), (-1, -1), (0, -1), (1, -1), (-1, 1), (0, 1), (1, 1))
SLOTS = M + SUB
HALO_ROWS = 24
HALO_ROOM = 40


def fresh_units():
    units = [((0, 0, 0), (SUB, 0, 0))]
    for lag in range(1, M):
        for first in range(0, M - lag, SUB):
            units.append(((first, lag, 0), (first, lag, 1)))
    return units


def field_of(units):
    table = {}
    for index, unit in enumerate(units):
        for half, (first, lag, part) in enumerate(unit):
            for lane in range(SUB):
                i = first + lane
                if i + lag < M:
                    table[(i, i + lag, part)] = index * 2 * SUB + half * SUB + lane
    return table


FRESH = fresh_units()
FIELDS = field_of(FRESH)


def window_sums(lines, outputs):
    core = lines[outputs - 1]
    for e in range(outputs, WIN):
        core = core + lines[e]
    low = [None] * outputs
    low[outputs - 1] = core
    for r in range(outputs - 2, -1, -1):
        low[r] = low[r + 1] + lines[r]
    sums = [low[0]]
    high = None
    for r in range(1, outputs):
        extra = lines[WIN - 1 + r]
        high = extra if high is None else high + extra
        sums.append(low[r] + high)
    return sums


def split(value):
    high = value.astype(jnp.bfloat16)
    low = (value - high.astype(jnp.float32)).astype(jnp.bfloat16)
    return high, low


def kernel(
    row_count,
    col_count,
    direct,
    slc_hbm,
    land_hbm,
    linked,
    comp_out,
    strength,
    slc,
    land,
    sig,
    up,
    dn,
    pack_send,
    pack_recv,
    halo,
    comp_send,
    comp_up,
    comp_dn,
    cpack_send,
    cpack_recv,
    w_main,
    w_halo,
    ybuf,
    hbuf,
    zbuf,
    ycbuf,
    hcbuf,
    zcbuf,
    coh,
    part,
    red_row,
    red_col,
    load_sem,
    ready,
    send_a,
    recv_a,
    send_b,
    recv_b,
    send_r,
    recv_r,
    send_c,
    recv_c,
):
    rows, cols = land.shape
    my_row = lax.axis_index("row")
    my_col = lax.axis_index("col")
    strip = rows * REACH
    loads = [
        pltpu.make_async_copy(slc_hbm, slc, load_sem.at[0]),
        pltpu.make_async_copy(land_hbm, land, load_sem.at[1]),
    ]
    for load in loads:
        load.start()

    exists = []
    for dr, dc in AROUND:
        ok = None
        for pos, step, count in ((my_row, dr, row_count), (my_col, dc, col_count)):
            if step:
                here = (pos > 0) if step < 0 else (pos < count - 1)
                ok = here if ok is None else jnp.logical_and(ok, here)
        exists.append(ok)

    for k, (dr, dc) in enumerate(AROUND):

        @pl.when(jnp.logical_not(exists[k]))
        def _(k=k, dc=dc, dr=dr):
            if dc == 0:
                target, small = (up, comp_up) if dr < 0 else (dn, comp_dn)
                for m in range(MS):
                    target[m] = jnp.zeros(target.shape[1:], jnp.float32)
                small[...] = jnp.zeros_like(small)
            else:
                for m in range(MS):
                    pack_recv[m, k - 2] = jnp.zeros(pack_recv.shape[2:], jnp.float32)
                cpack_recv[k - 2] = jnp.zeros(cpack_recv.shape[1:], jnp.float32)

    barrier = pltpu.get_barrier_semaphore()
    mesh_id = pl.DeviceIdType.MESH
    expected = jnp.int32(row_count - 1 + col_count - 1)
    for step in range(1, row_count):
        pl.semaphore_signal(
            barrier, inc=1, device_id=(lax.rem(my_row + step, row_count), my_col), device_id_type=mesh_id
        )
    for step in range(1, col_count):
        pl.semaphore_signal(
            barrier, inc=1, device_id=(my_row, lax.rem(my_col + step, col_count)), device_id_type=mesh_id
        )
    for k, (dr, dc) in enumerate(AROUND):
        if dr and dc:

            @pl.when(exists[k])
            def _(dr=dr, dc=dc):
                pl.semaphore_signal(
                    barrier, inc=1, device_id=(my_row + dr, my_col + dc), device_id_type=mesh_id
                )

            expected = expected + exists[k].astype(jnp.int32)

    for load in loads:
        load.wait()
    mask = land[...].astype(jnp.float32)
    for m in range(MS):
        for i in range(M):
            for c in range(2):
                at = (i * 2 + c) * rows
                sig[m, at : at + rows, :] = slc[m * M + i, c] * mask
        for buffer in (sig, up, dn):
            buffer[m, M * 2 * rows :, :] = jnp.zeros((buffer.shape[1] - M * 2 * rows, cols), jnp.float32)

    lane = lax.broadcasted_iota(jnp.int32, (rows, cols), 1)
    sub = lax.broadcasted_iota(jnp.int32, (rows, cols), 0)
    from_right = (lane >= sub * REACH) & (lane < sub * REACH + REACH)
    from_left = (lane >= (sub + 1) * REACH) & (lane < (sub + 2) * REACH)

    def pack_tile(tile):
        turned = pltpu.roll(tile, REACH, 1, stride=REACH, stride_axis=0)
        high = jnp.sum(jnp.where(from_right, turned, 0.0), axis=0, keepdims=True)
        low = jnp.sum(jnp.where(from_left, turned, 0.0), axis=0, keepdims=True)
        return low, high

    def spread(line, shift):
        total = pltpu.roll(line, cols - shift, 1) if shift else line
        return (
            total
            + pltpu.roll(line, (strip - shift) % cols, 1)
            + pltpu.roll(line, (2 * strip - shift) % cols, 1)
        )

    for m in range(MS):
        pack_send[m] = jnp.zeros(pack_send.shape[1:], jnp.float32)
        for i in range(M):
            for c in range(2):
                low, high = pack_tile(sig[m, (i * 2 + c) * rows : (i * 2 + c + 1) * rows, :])
                pack_send[m, 0, c * (M + 1) + i : c * (M + 1) + i + 1, :] = low
                pack_send[m, 1, c * (M + 1) + i : c * (M + 1) + i + 1, :] = high
        pack_send[m, 0] = spread(pack_send[m, 0], REACH)
        pack_send[m, 1] = spread(pack_send[m, 1], 0)
        pack_recv[m, :, HALO_ROWS:, :] = jnp.zeros((6, HALO_ROOM - HALO_ROWS, cols), jnp.float32)

    pl.semaphore_wait(barrier, expected)

    def mirror(k):
        dr, dc = AROUND[k]
        return AROUND.index((-dr, -dc))

    def fresh_copy(m, k):
        dr, dc = AROUND[k]
        back = mirror(k)
        if dc == 0:
            source = sig.at[m, pl.ds(0, M * 2 * rows)]
            target = (dn if dr < 0 else up).at[m, pl.ds(0, M * 2 * rows)]
        else:
            source = pack_send.at[m, 0 if dc < 0 else 1]
            target = pack_recv.at[m, back - 2, pl.ds(0, HALO_ROWS)]
        return pltpu.make_async_remote_copy(
            src_ref=source,
            dst_ref=target,
            send_sem=send_a.at[m, k],
            recv_sem=recv_a.at[m, back],
            device_id=(my_row + dr, my_col + dc),
            device_id_type=mesh_id,
        )

    def fresh_arrival(m, k):
        dr, dc = AROUND[k]
        if dc == 0:
            source = sig.at[m, pl.ds(0, M * 2 * rows)]
            target = (up if dr < 0 else dn).at[m, pl.ds(0, M * 2 * rows)]
        else:
            source = pack_send.at[m, 0 if dc < 0 else 1]
            target = pack_recv.at[m, k - 2, pl.ds(0, HALO_ROWS)]
        return pltpu.make_async_remote_copy(
            src_ref=source,
            dst_ref=target,
            send_sem=send_a.at[m, k],
            recv_sem=recv_a.at[m, k],
            device_id=(my_row + dr, my_col + dc),
            device_id_type=mesh_id,
        )

    def each_around(action):
        for k in range(len(AROUND)):

            @pl.when(exists[k])
            def _(k=k):
                action(k)

    for m in range(MS):
        each_around(lambda k, m=m: fresh_copy(m, k).start())

    if direct:
        for step in range(1, col_count):
            pl.semaphore_signal(
                ready, inc=1, device_id=(my_row, lax.rem(my_col + step, col_count)), device_id_type=mesh_id
            )

    k_at = lax.broadcasted_iota(jnp.int32, (cols, cols), 0)
    n_at = lax.broadcasted_iota(jnp.int32, (cols, cols), 1)
    near = jnp.where((k_at - n_at <= REACH) & (n_at - k_at <= REACH), 1.0, 0.0).astype(jnp.bfloat16)
    w_main[0:cols, :] = near
    w_main[cols:, :] = near
    line_of = k_at // REACH
    inner = k_at - line_of * REACH
    for side in range(2):
        touches = (n_at <= inner) if side == 0 else (n_at >= inner + cols - REACH)
        line = jnp.where(touches, line_of, -1)
        for r in range(rows):
            first = rows - REACH + r
            w_halo[side * cols : (side + 1) * cols, r * cols : (r + 1) * cols] = jnp.where(
                (line >= first) & (line < first + WIN), 1.0, 0.0
            ).astype(jnp.bfloat16)

    outer = (up, sig, dn)
    lane_halo = lax.broadcasted_iota(jnp.int32, (HALO_ROOM, cols), 1)

    def gather_halo(m, parts, target):
        for side in range(2):
            a, b, c = (parts(side * 3 + j) for j in range(3))
            which = lane_halo[: a.shape[0]]
            target(side, jnp.where(which < strip, a, jnp.where(which < 2 * strip, b, c)))

    def line_tile(m, e, c, first):
        at = rows - REACH + e
        buffer = outer[at // rows]
        return buffer[m, pl.ds((first * 2 + c) * rows + at % rows, SUB, stride=2 * rows), :]

    def halo_tile(m, side, c, first):
        at = c * (M + 1) + first
        return halo[m, side, at : at + SUB, :]

    def emit(index, halves, ytarget, htarget):
        lines_total = WIN + rows - 1
        both = [jnp.concatenate([x, y], 0) for x, y in zip(halves[0], halves[1])]
        at = slice(index * 2 * SUB, (index + 1) * 2 * SUB)
        for r, total in enumerate(window_sums(both[:lines_total], rows)):
            high, low = split(total)
            ytarget[r, at, 0:cols] = high
            ytarget[r, at, cols:] = low
        for side in range(2):
            high, low = split(both[lines_total + side])
            htarget[0, at, side * cols : (side + 1) * cols] = high
            htarget[1, at, side * cols : (side + 1) * cols] = low

    def sources(m):
        lines_total = WIN + rows - 1
        return [functools.partial(line_tile, m, e) for e in range(lines_total)] + [
            functools.partial(halo_tile, m, side) for side in range(2)
        ]

    def real_part(a, b, x, y):
        return a * x + b * y

    def imag_part(a, b, x, y):
        return b * x - a * y

    def fresh_fields(m):
        for index, unit in enumerate(FRESH):
            halves = ([], [])
            for tile in sources(m):
                if index == 0:
                    for half in range(2):
                        first = unit[half][0]
                        a, b = tile(0, first), tile(1, first)
                        halves[half].append(a * a + b * b)
                else:
                    first, lag, _ = unit[0]
                    a, b = tile(0, first), tile(1, first)
                    x, y = tile(0, first + lag), tile(1, first + lag)
                    halves[0].append(real_part(a, b, x, y))
                    halves[1].append(imag_part(a, b, x, y))
            emit(index, halves, ybuf, hbuf)

    def windowed(ysource, hsource, target):
        count = ysource.shape[1]
        main = jnp.dot(
            ysource[...].reshape(rows * count, 2 * cols), w_main[...], preferred_element_type=jnp.float32
        )
        for r in range(rows):
            band = w_halo[:, r * cols : (r + 1) * cols]
            edge = jnp.dot(hsource[0], band, preferred_element_type=jnp.float32) + jnp.dot(
                hsource[1], band, preferred_element_type=jnp.float32
            )
            target[r * count : (r + 1) * count, :] = main[r * count : (r + 1) * count, :] + edge

    fresh_count = len(FRESH) * 2 * SUB

    def fresh_field(i, j, p):
        return zbuf[pl.ds(FIELDS[(i, j, p)], rows, stride=fresh_count), :]

    def power(number, field):
        scales = [
            lax.rsqrt(jnp.maximum(field(i, i, 0), covariance_floor)) for i in range(number)
        ]
        vec_re = [None] * number
        vec_im = [None] * number

        def add(store, i, value):
            store[i] = value if store[i] is None else store[i] + value

        def sub_(store, i, value):
            store[i] = -value if store[i] is None else store[i] - value

        slot = {}
        next_slot = 0
        for i in range(number):
            c = field(i, i, 0) * (scales[i] * scales[i])
            coh[next_slot] = c
            slot[(i, i, 0)] = next_slot
            next_slot += 1
            add(vec_re, i, c)
            for j in range(i + 1, number):
                s = scales[i] * scales[j]
                c = field(i, j, 0) * s
                d = field(i, j, 1) * s
                coh[next_slot] = c
                coh[next_slot + 1] = d
                slot[(i, j, 0)] = next_slot
                slot[(i, j, 1)] = next_slot + 1
                next_slot += 2
                add(vec_re, i, c)
                add(vec_re, j, c)
                add(vec_im, i, d)
                sub_(vec_im, j, d)

        def normalise():
            squares = None
            for i in range(number):
                both = vec_re[i] * vec_re[i] + vec_im[i] * vec_im[i]
                squares = both if squares is None else squares + both
            length = jnp.sqrt(squares)
            inverse = 1.0 / jnp.maximum(length, 1.0)
            return length, [v * inverse for v in vec_re], [v * inverse for v in vec_im]

        length, old_re, old_im = normalise()
        for _ in range(1, ITERS):
            vec_re = [None] * number
            vec_im = [None] * number
            for i in range(number):
                c = coh[slot[(i, i, 0)]]
                add(vec_re, i, c * old_re[i])
                add(vec_im, i, c * old_im[i])
                for j in range(i + 1, number):
                    c = coh[slot[(i, j, 0)]]
                    d = coh[slot[(i, j, 1)]]
                    add(vec_re, i, c * old_re[j] - d * old_im[j])
                    add(vec_im, i, c * old_im[j] + d * old_re[j])
                    add(vec_re, j, c * old_re[i] + d * old_im[i])
                    add(vec_im, j, c * old_im[i] - d * old_re[i])
            length, old_re, old_im = normalise()
        return length, old_re, old_im

    def finish(m, number, field):
        length, re, im = power(number, field)
        re, im = re[number - M :], im[number - M :]
        comp_re = comp_im = None
        for i in range(M):
            a = sig[m, i * 2 * rows : (i * 2 + 1) * rows, :]
            b = sig[m, (i * 2 + 1) * rows : (i * 2 + 2) * rows, :]
            x = re[i] * a + im[i] * b
            y = re[i] * b - im[i] * a
            comp_re = x if comp_re is None else comp_re + x
            comp_im = y if comp_im is None else comp_im + y
            linked[m * M + i, 0] = re[i] * mask
            linked[m * M + i, 1] = im[i] * mask
        share = jnp.sum(mask * length, axis=0, keepdims=True) * (1.0 / number)
        share = share + pltpu.roll(share, cols // 2, 1)
        lane_line = lax.broadcasted_iota(jnp.int32, (1, cols), 1)
        if m == 0:
            part[...] = share
        else:
            part[...] = jnp.where(lane_line < cols // 2, part[...], share)
        return comp_re, comp_im

    def take_fresh(m):
        each_around(lambda k: fresh_arrival(m, k).wait_recv())

        def put(side, value):
            halo[m, side] = value

        gather_halo(m, lambda j: pack_recv[m, j], put)

    take_fresh(0)
    fresh_fields(0)
    windowed(ybuf, hbuf, zbuf)
    comp_re, comp_im = finish(0, M, fresh_field)
    comp_send[0:rows, :] = comp_re
    comp_send[rows:, :] = comp_im
    cpack_send[...] = jnp.zeros_like(cpack_send)
    for c, value in enumerate((comp_re, comp_im)):
        low, high = pack_tile(value)
        cpack_send[0, c : c + 1, :] = spread(low, REACH)
        cpack_send[1, c : c + 1, :] = spread(high, 0)

    def comp_pair(k, sending):
        dr, dc = AROUND[k]
        slot = mirror(k) if sending else k
        if dc == 0:
            source = comp_send
            target = comp_up if AROUND[slot][0] < 0 else comp_dn
        else:
            source = cpack_send.at[0 if dc < 0 else 1]
            target = cpack_recv.at[slot - 2]
        return pltpu.make_async_remote_copy(
            src_ref=source,
            dst_ref=target,
            send_sem=send_b.at[k],
            recv_sem=recv_b.at[slot],
            device_id=(my_row + dr, my_col + dc),
            device_id_type=mesh_id,
        )

    each_around(lambda k: comp_pair(k, True).start())

    last = MS - 1
    take_fresh(last)
    fresh_fields(last)
    windowed(ybuf, hbuf, zbuf)

    each_around(lambda k: comp_pair(k, False).wait_recv())
    at = M * 2 * rows
    sig[last, at : at + 2 * rows, :] = comp_send[...]
    up[last, at : at + 2 * rows, :] = comp_up[...]
    dn[last, at : at + 2 * rows, :] = comp_dn[...]

    def put_comp(side, value):
        for c in range(2):
            row = c * (M + 1) + M
            halo[last, side, row : row + 1, :] = value[c : c + 1]

    gather_halo(last, lambda j: cpack_recv[j], put_comp)

    for index, first in enumerate(range(0, M + 1, SUB)):
        halves = ([], [])
        for tile_at in range(WIN + rows - 1 + 2):
            if tile_at < WIN + rows - 1:
                pos = rows - REACH + tile_at
                buffer = outer[pos // rows]
                base = M * 2 * rows + pos % rows
                a = buffer[last, base : base + 1, :]
                b = buffer[last, base + rows : base + rows + 1, :]
            else:
                side = tile_at - (WIN + rows - 1)
                a = halo[last, side, M : M + 1, :]
                b = halo[last, side, 2 * M + 1 : 2 * M + 2, :]
            a = jnp.broadcast_to(a, (SUB, cols))
            b = jnp.broadcast_to(b, (SUB, cols))
            tile = sources(last)[tile_at]
            x, y = tile(0, first), tile(1, first)
            halves[0].append(real_part(a, b, x, y))
            halves[1].append(imag_part(a, b, x, y))
        emit(index, halves, ycbuf, hcbuf)
    windowed(ycbuf, hcbuf, zcbuf)
    comp_count = ycbuf.shape[1]

    def last_field(i, j, p):
        if i > 0:
            return fresh_field(i - 1, j - 1, p)
        other = M if j == 0 else j - 1
        at = (other // SUB) * 2 * SUB + p * SUB + other % SUB
        return zcbuf[pl.ds(at, rows, stride=comp_count), :]

    comp_re, comp_im = finish(last, M + 1, last_field)
    comp_out[0] = comp_re
    comp_out[1] = comp_im

    def reduce(count, me, device, source, buffer, sends, recvs):
        copies = []
        for step in range(1, count):
            copy = pltpu.make_async_remote_copy(
                src_ref=source,
                dst_ref=buffer.at[me],
                send_sem=sends.at[step],
                recv_sem=recvs.at[me],
                device_id=device(lax.rem(me + step, count)),
                device_id_type=mesh_id,
            )
            copy.start()
            copies.append(copy)
        buffer[me] = source[...]
        for step in range(1, count):
            other = lax.rem(me + step, count)
            pltpu.make_async_remote_copy(
                src_ref=source,
                dst_ref=buffer.at[other],
                send_sem=sends.at[step],
                recv_sem=recvs.at[other],
                device_id=device(other),
                device_id_type=mesh_id,
            ).wait_recv()
        for copy in copies:
            copy.wait_send()
        total = buffer[0]
        for other in range(1, count):
            total = total + buffer[other]
        return total

    if direct:
        pl.semaphore_wait(ready, col_count - 1)
        me = my_row * col_count + my_col
        total = reduce(
            row_count * col_count, me, lambda d: (d // col_count, d % col_count), part, red_row, send_r, recv_r
        )
    else:
        total = reduce(row_count, my_row, lambda d: (d, my_col), part, red_row, send_r, recv_r)
        part2 = red_col.at[col_count]
        part2[...] = total
        total = reduce(col_count, my_col, lambda d: (my_row, d), part2, red_col, send_c, recv_c)
    strength[...] = total

    for m in range(MS):
        each_around(lambda k, m=m: fresh_copy(m, k).wait_send())
    each_around(lambda k: comp_pair(k, True).wait_send())


def closing(pixels, linked_in, comp_in, total, linked, comp, strength, sems):
    copies = [
        pltpu.make_async_copy(linked_in, linked, sems.at[0]),
        pltpu.make_async_copy(comp_in, comp, sems.at[1]),
    ]
    for copy in copies:
        copy.start()
    for m in range(MS):
        lane = lax.broadcasted_iota(jnp.int32, total.shape, 1)
        mine = lane < total.shape[1] // 2 if m == 0 else lane >= total.shape[1] // 2
        strength[m] = jnp.sum(jnp.where(mine, total[...], 0.0)) / pixels
    for copy in copies:
        copy.wait()


def shards(slc_stack, land_mask):
    rows, cols = land_mask.shape
    row_count, col_count = lax.axis_size("row"), lax.axis_size("col")
    f32, bf16 = jnp.float32, jnp.bfloat16
    images = (MS, SLOTS * 2 * rows, cols)
    fresh_count = len(FRESH) * 2 * SUB
    comp_count = 2 * SUB * (-(-(M + 1) // SUB))
    vmem = pl.BlockSpec(memory_space=pltpu.VMEM)
    dma = pltpu.SemaphoreType.DMA
    hbm = pl.BlockSpec(memory_space=pltpu.HBM)
    devices = row_count * col_count
    direct = devices <= 64
    peers = devices if direct else row_count
    linked_shape = jax.ShapeDtypeStruct(slc_stack.shape, f32)
    comp_shape = jax.ShapeDtypeStruct((2, rows, cols), f32)
    linked, comp, total = pl.pallas_call(
        functools.partial(kernel, row_count, col_count, direct),
        out_shape=(linked_shape, comp_shape, jax.ShapeDtypeStruct((1, cols), f32)),
        in_specs=[hbm, hbm],
        out_specs=(vmem, vmem, vmem),
        scratch_shapes=[
            pltpu.VMEM(slc_stack.shape, f32),
            pltpu.VMEM((rows, cols), jnp.int32),
            pltpu.VMEM(images, f32),
            pltpu.VMEM(images, f32),
            pltpu.VMEM(images, f32),
            pltpu.VMEM((MS, 2, HALO_ROWS, cols), f32),
            pltpu.VMEM((MS, 6, HALO_ROOM, cols), f32),
            pltpu.VMEM((MS, 2, HALO_ROOM, cols), f32),
            pltpu.VMEM((2 * rows, cols), f32),
            pltpu.VMEM((2 * rows, cols), f32),
            pltpu.VMEM((2 * rows, cols), f32),
            pltpu.VMEM((2, SUB, cols), f32),
            pltpu.VMEM((6, SUB, cols), f32),
            pltpu.VMEM((2 * cols, cols), bf16),
            pltpu.VMEM((2 * cols, rows * cols), bf16),
            pltpu.VMEM((rows, fresh_count, 2 * cols), bf16),
            pltpu.VMEM((2, fresh_count, 2 * cols), bf16),
            pltpu.VMEM((rows * fresh_count, cols), f32),
            pltpu.VMEM((rows, comp_count, 2 * cols), bf16),
            pltpu.VMEM((2, comp_count, 2 * cols), bf16),
            pltpu.VMEM((rows * comp_count, cols), f32),
            pltpu.VMEM(((M + 1) * (M + 1), rows, cols), f32),
            pltpu.VMEM((1, cols), f32),
            pltpu.VMEM((peers, 1, cols), f32),
            pltpu.VMEM((col_count + 1, 1, cols), f32),
            dma((2,)),
            pltpu.SemaphoreType.REGULAR,
            dma((MS, len(AROUND))),
            dma((MS, len(AROUND))),
            dma((len(AROUND),)),
            dma((len(AROUND),)),
            dma((peers,)),
            dma((peers,)),
            dma((col_count,)),
            dma((col_count,)),
        ],
        compiler_params=pltpu.CompilerParams(collective_id=0, has_side_effects=True, vmem_limit_bytes=16 << 20),
        name="linker",
    )(*(pltpu.with_memory_space_constraint(x, pltpu.HBM) for x in (slc_stack, land_mask)))
    return pl.pallas_call(
        functools.partial(closing, rows * cols * devices),
        out_shape=(linked_shape, comp_shape, jax.ShapeDtypeStruct((MS,), f32)),
        in_specs=[vmem, vmem, vmem],
        out_specs=(hbm, hbm, pl.BlockSpec(memory_space=pltpu.SMEM)),
        scratch_shapes=[dma((2,))],
        compiler_params=pltpu.CompilerParams(vmem_limit_bytes=4 << 20),
        name="closing",
    )(linked, comp, total)


def solution(mesh):
    return jax.shard_map(
        shards,
        mesh=mesh,
        in_specs=(P(None, None, "row", "col"), P("row", "col")),
        out_specs=(P(None, None, "row", "col"), P(None, "row", "col"), P()),
        check_vma=False,
    )
```

profile of v0, /device:TPU:0, one launch (start us, length us, event | category | flops | bytes accessed | tf_op | source)
XLA Modules:
  0.0 23.9 jit_solution(5366835162707014717)
XLA Ops:
  0.6 22.0 %linker.1 = (f32[20,2,8,128]{3,2,1,0:T(8,128)S(1)}, f32[2,8,128]{2,1,0:T(8,128)S(1)}, f32[1,128]{1,0:T(1,128)S(1)}) custom-call(f32[20,2,8,128]{3,2,1,0:T(8,128)} %slc_hbm.1, s32[8,128]{1,0:T(8,128)} %land_hbm.1), custom_call_target="tpu_custom_call" | custom-call | tf_op jit(solution)/shard_map/linker/pallas_call | solution.py:618
  22.7 1.2 %closing.1 = (f32[20,2,8,128]{3,2,1,0:T(8,128)}, f32[2,8,128]{2,1,0:T(8,128)}, f32[2]{0:T(128)}) custom-call(f32[20,2,8,128]{3,2,1,0:T(8,128)S(1)} %get-tuple-element.6.linked_in, f32[2,8,128]{2,1,0:T(8,128)S(1)} %get-tuple-element.7.comp_in, f32[1,128]{1,0:T(1,128)S(1)} %get-tuple-element.8.total), custom_call_target="tpu_custom_call" | custom-call | tf_op jit(solution)/shard_map/closing/pallas_call | solution.py:663
where the time goes:
time: 24 us; the launch traced here: 23.9 us
  Pallas kernels  23.2 us (97%)
  between operations  0.64 us (3%)
    pallas_call x1, Pallas kernels, shards(): pl.pallas_call(functools.partial(kernel, row_count, col_count, direct), o...  22 us
    pallas_call x1, Pallas kernels, shards(): pl.pallas_call(functools.partial(closing, rows * cols * devices), out_sha...  1.2 us

commit v1 on v0

v1 whole, which is shorter than its diff:
```python
import functools

import jax
import jax.numpy as jnp
from jax import lax
from jax.experimental import pallas as pl
from jax.experimental.pallas import tpu as pltpu
from jax.sharding import PartitionSpec as P

M = 10
MS = 2
WIN = 11
ITERS = 4
REACH = WIN // 2
SUB = 8

covariance_floor = 8.0

AROUND = ((-1, 0), (1, 0), (-1, -1), (0, -1), (1, -1), (-1, 1), (0, 1), (1, 1))
LINE = 2 * M
EDGE = -(-REACH * LINE // SUB) * SUB
SKIP = EDGE - REACH * LINE
PACK = -(-LINE // SUB) * SUB


def pair_groups():
    groups = [[(s, (s + lag) % SUB) for s in range(SUB)] for lag in range(1, SUB // 2)]
    half = SUB // 2
    groups.append([(s, s + half) for s in range(half)] + [(M - 2, M - 1), (M - 2, M - 2), (M - 1, M - 1)])
    groups.append([(s, M - 2) for s in range(SUB)])
    groups.append([(s, M - 1) for s in range(SUB)])
    groups.append([(s, s) for s in range(SUB)])
    return groups


def field_rows(groups):
    table = {}
    for unit, group in enumerate(groups):
        for lane, (i, j) in enumerate(group):
            for part in range(1 if i == j else 2):
                table[(i, j, part)] = unit * 2 * SUB + part * SUB + lane
    return table


GROUPS = pair_groups()
LATE = [[(s, M) for s in range(SUB)], [(M, M)] * (2 * SUB - M) + [(s, M) for s in range(SUB, M)]]
FIELDS = field_rows(GROUPS)
LATE_FIELDS = field_rows(LATE)
PAIRS = [(i, j) for i, j, part in FIELDS if part == 1]
LATE_PAIRS = [(i, j) for i, j, part in LATE_FIELDS if part == 1]
FRESH_ROWS = len(GROUPS) * 2 * SUB
LATE_ROWS = len(LATE) * 2 * SUB
FRESH_STEP = FRESH_ROWS + 4
LATE_STEP = LATE_ROWS + 4
SLOTS = 3 * (len(PAIRS) + len(LATE_PAIRS)) + M + 1


def window_sums(lines, outputs):
    core = lines[outputs - 1]
    for e in range(outputs, WIN):
        core = core + lines[e]
    low = [None] * outputs
    low[outputs - 1] = core
    for r in range(outputs - 2, -1, -1):
        low[r] = low[r + 1] + lines[r]
    sums = [low[0]]
    high = None
    for r in range(1, outputs):
        extra = lines[WIN - 1 + r]
        high = extra if high is None else high + extra
        sums.append(low[r] + high)
    return sums


def split(value):
    high = value.astype(jnp.bfloat16)
    low = (value - high.astype(jnp.float32)).astype(jnp.bfloat16)
    return high, low


def waves(row_count, col_count):
    offsets = []
    known = 1
    while known < max(row_count, col_count) - 1:
        offsets.append(known)
        known *= 2
    return offsets


def kernel(
    row_count,
    col_count,
    direct,
    slc_hbm,
    land_hbm,
    linked,
    comp_out,
    strength,
    slc,
    land,
    own,
    up,
    dn,
    pack_send,
    pack_recv,
    halo,
    comp_send,
    comp_up,
    comp_dn,
    cpack_send,
    cpack_recv,
    chalo,
    w_main,
    w_halo,
    ybuf,
    hbuf,
    ebuf,
    zbuf,
    zcbuf,
    coh,
    part,
    red_row,
    red_col,
    load_sem,
    ready,
    send_a,
    recv_a,
    send_b,
    recv_b,
    send_r,
    recv_r,
    send_c,
    recv_c,
):
    rows, cols = land.shape
    my_row = lax.axis_index("row")
    my_col = lax.axis_index("col")
    strip = rows * REACH
    mesh_id = pl.DeviceIdType.MESH
    loads = [
        pltpu.make_async_copy(slc_hbm, slc, load_sem.at[0]),
        pltpu.make_async_copy(land_hbm, land, load_sem.at[1]),
    ]
    for load in loads:
        load.start()

    def existing(dr, dc, far=1):
        ok = None
        for pos, step, count in ((my_row, dr, row_count), (my_col, dc, col_count)):
            if step:
                here = (pos >= far) if step < 0 else (pos < count - far)
                ok = here if ok is None else jnp.logical_and(ok, here)
        return ok

    exists = [existing(dr, dc) for dr, dc in AROUND]

    def greet(semaphore, far):
        expected = jnp.int32(0)
        for k, (dr, dc) in enumerate(AROUND):
            if (dr and far >= row_count) or (dc and far >= col_count):
                continue
            there = existing(dr, dc, far)

            @pl.when(there)
            def _(dr=dr, dc=dc):
                pl.semaphore_signal(
                    semaphore,
                    inc=1,
                    device_id=(my_row + dr * far, my_col + dc * far),
                    device_id_type=mesh_id,
                )

            expected = expected + there.astype(jnp.int32)
        return expected

    barrier = pltpu.get_barrier_semaphore()
    expected = greet(barrier, 1)
    offsets = waves(row_count, col_count)
    pending = []

    def next_wave():
        if pending:
            index, count = pending.pop()
            pl.semaphore_wait(ready.at[index], count)
            index += 1
        else:
            index = 0
        if index < len(offsets):
            pending.append((index, greet(ready.at[index], offsets[index])))

    for k, (dr, dc) in enumerate(AROUND):

        @pl.when(jnp.logical_not(exists[k]))
        def _(k=k, dc=dc, dr=dr):
            if dc == 0:
                target, small = (up, comp_up) if dr < 0 else (dn, comp_dn)
                for m in range(MS):
                    target[m] = jnp.zeros(target.shape[1:], jnp.float32)
                small[...] = jnp.zeros_like(small)
            else:
                for m in range(MS):
                    pack_recv[m, k - 2] = jnp.zeros(pack_recv.shape[2:], jnp.float32)
                cpack_recv[k - 2] = jnp.zeros(cpack_recv.shape[1:], jnp.float32)

    lane = lax.broadcasted_iota(jnp.int32, (rows, cols), 1)
    sub = lax.broadcasted_iota(jnp.int32, (rows, cols), 0)

    for load in loads:
        load.wait()
    mask = land[...].astype(jnp.float32)

    def place(m):
        for i in range(M):
            for c in range(2):
                own[m, pl.ds(c * M + i, rows, stride=LINE), :] = slc[m * M + i, c] * mask
        own[m, rows * LINE :, :] = jnp.zeros((own.shape[1] - rows * LINE, cols), jnp.float32)

    def spread(line, shift):
        total = pltpu.roll(line, cols - shift, 1) if shift else line
        return (
            total
            + pltpu.roll(line, (strip - shift) % cols, 1)
            + pltpu.roll(line, (2 * strip - shift) % cols, 1)
        )

    def pack(m):
        for at in range(0, PACK, SUB):
            low = high = jnp.zeros((SUB, cols), jnp.float32)
            for r in range(rows):
                turned = pltpu.roll(own[m, r * LINE + at : r * LINE + at + SUB, :], REACH * (r + 1), 1)
                high = jnp.where((lane >= r * REACH) & (lane < (r + 1) * REACH), turned, high)
                low = jnp.where((lane >= (r + 1) * REACH) & (lane < (r + 2) * REACH), turned, low)
            pack_send[m, 0, at : at + SUB, :] = spread(low, REACH)
            pack_send[m, 1, at : at + SUB, :] = spread(high, 0)

    def mirror(k):
        dr, dc = AROUND[k]
        return AROUND.index((-dr, -dc))

    def fresh_pair(m, k, sending):
        dr, dc = AROUND[k]
        back = mirror(k)
        slot = back if sending else k
        if dc == 0:
            source = own.at[m, pl.ds(0 if dr < 0 else rows * LINE - EDGE, EDGE)]
            target = (up if AROUND[slot][0] < 0 else dn).at[m, pl.ds(0, EDGE)]
        else:
            source = pack_send.at[m, 0 if dc < 0 else 1]
            target = pack_recv.at[m, slot - 2]
        return pltpu.make_async_remote_copy(
            src_ref=source,
            dst_ref=target,
            send_sem=send_a.at[m, k],
            recv_sem=recv_a.at[m, slot],
            device_id=(my_row + dr, my_col + dc),
            device_id_type=mesh_id,
        )

    def each_around(action):
        for k in range(len(AROUND)):

            @pl.when(exists[k])
            def _(k=k):
                action(k)

    place(0)
    pack(0)
    pl.semaphore_wait(barrier, expected)
    each_around(lambda k: fresh_pair(0, k, True).start())
    for m in range(1, MS):
        place(m)
        pack(m)
        each_around(lambda k, m=m: fresh_pair(m, k, True).start())
    next_wave()

    k_at = lax.broadcasted_iota(jnp.int32, (cols, cols), 0)
    n_at = lax.broadcasted_iota(jnp.int32, (cols, cols), 1)
    near = jnp.where((k_at - n_at <= REACH) & (n_at - k_at <= REACH), 1.0, 0.0).astype(jnp.bfloat16)
    w_main[0:cols, :] = near
    w_main[cols:, :] = near
    line_of = k_at // REACH
    inner = k_at - line_of * REACH
    for side in range(2):
        touches = (n_at <= inner) if side == 0 else (n_at >= inner + cols - REACH)
        line = jnp.where(touches, line_of, -1)
        for r in range(rows):
            first = rows - REACH + r
            w_halo[side * cols : (side + 1) * cols, r * cols : (r + 1) * cols] = jnp.where(
                (line >= first) & (line < first + WIN), 1.0, 0.0
            ).astype(jnp.bfloat16)

    lines_total = WIN + rows - 1

    def gather_halo(parts):
        sides = []
        for side in range(2):
            a, b, c = (parts(side * 3 + j) for j in range(3))
            which = lax.broadcasted_iota(jnp.int32, a.shape, 1)
            sides.append(jnp.where(which < strip, a, jnp.where(which < 2 * strip, b, c)))
        return sides

    def line_tile(m, e, c, first):
        if e < REACH:
            buffer, at = up, SKIP + e * LINE
        elif e < REACH + rows:
            buffer, at = own, (e - REACH) * LINE
        else:
            buffer, at = dn, (e - REACH - rows) * LINE
        at += c * M + first
        return buffer[m, at : at + SUB, :]

    def halo_tile(m, side, c, first):
        at = c * M + first
        return halo[m, side, at : at + SUB, :]

    def real_part(a, b, x, y):
        return a * x + b * y

    def imag_part(a, b, x, y):
        return b * x - a * y

    def operands(tile, unit):
        lead = [tile(c, 0) for c in range(2)]
        if unit < SUB // 2 - 1:
            return lead, [pltpu.roll(v, SUB - 1 - unit, 0) for v in lead]
        if unit == SUB // 2 - 1:
            left, right = [], []
            for c in range(2):
                mid, late = tile(c, SUB // 2), tile(c, SUB - M + 5)
                left.append(jnp.where(sub < 4, lead[c], jnp.where(sub == 4, mid, late)))
                right.append(jnp.where(sub < 4, mid, jnp.where(sub == 4, tile(c, 5), late)))
            return left, right
        return lead, None

    def products(tile, row_tile, unit):
        (a, b), other = operands(tile, unit)
        if unit == len(GROUPS) - 1:
            return a * a + b * b, None
        if other is None:
            image = M - 2 + unit - SUB // 2
            x, y = (jnp.broadcast_to(row_tile(c, image), (SUB, cols)) for c in range(2))
        else:
            x, y = other
        return real_part(a, b, x, y), imag_part(a, b, x, y)

    def tile_of(m, e):
        if e < lines_total:
            return functools.partial(line_tile, m, e)
        return functools.partial(halo_tile, m, e - lines_total)

    def row_of(m, e):
        tile = tile_of(m, e)
        return lambda c, image: tile(c, image)[0:1]

    def emit_side(unit, side, value):
        high, low = split(value)
        at = slice(unit * 2 * SUB, (unit + 1) * 2 * SUB)
        hbuf[0, at, side * cols : (side + 1) * cols] = high
        hbuf[1, at, side * cols : (side + 1) * cols] = low

    def edges(count):
        for r in range(0, rows, 2):
            band = w_halo[:, r * cols : (r + 2) * cols]
            value = jnp.dot(hbuf[0, 0:count], band, preferred_element_type=jnp.float32) + jnp.dot(
                hbuf[1, 0:count], band, preferred_element_type=jnp.float32
            )
            ebuf[r, 0:count] = value[:, 0:cols]
            ebuf[r + 1, 0:count] = value[:, cols:]

    def emit_lines(unit, lines, target, step):
        for r, total in enumerate(window_sums(lines, rows)):
            high, low = split(total)
            ybuf[unit, r * 2 * SUB : (r + 1) * 2 * SUB, 0:cols] = high
            ybuf[unit, r * 2 * SUB : (r + 1) * 2 * SUB, cols:] = low
        main = jnp.dot(ybuf[unit], w_main[...], preferred_element_type=jnp.float32)
        for r in range(rows):
            at = r * step + unit * 2 * SUB
            target[at : at + 2 * SUB, :] = (
                main[r * 2 * SUB : (r + 1) * 2 * SUB, :] + ebuf[r, unit * 2 * SUB : (unit + 1) * 2 * SUB]
            )

    def both_halves(pair):
        first, second = pair
        return jnp.concatenate([first, jnp.zeros_like(first) if second is None else second], 0)

    def fresh_fields(m):
        for side in range(2):
            for unit in range(len(GROUPS)):
                e = lines_total + side
                emit_side(unit, side, both_halves(products(tile_of(m, e), row_of(m, e), unit)))
        edges(FRESH_ROWS)
        for unit in range(len(GROUPS)):
            lines = [both_halves(products(tile_of(m, e), row_of(m, e), unit)) for e in range(lines_total)]
            emit_lines(unit, lines, zbuf, FRESH_STEP)

    def comp_row(e, c):
        if e < REACH:
            at = c * rows + rows - REACH + e
            return comp_up[at : at + 1, :]
        if e < REACH + rows:
            at = c * rows + e - REACH
            return comp_send[at : at + 1, :]
        if e < lines_total:
            at = c * rows + e - REACH - rows
            return comp_dn[at : at + 1, :]
        return chalo[e - lines_total, c : c + 1, :]

    def late_products(m, e, unit):
        tile = tile_of(m, e)
        x, y = (jnp.broadcast_to(comp_row(e, c), (SUB, cols)) for c in range(2))
        if unit == 0:
            a, b = tile(0, 0), tile(1, 0)
        else:
            a, b = (jnp.where(sub < 2 * SUB - M, v, tile(c, M - SUB)) for c, v in enumerate((x, y)))
        return jnp.concatenate([real_part(a, b, x, y), imag_part(a, b, x, y)], 0)

    def late_fields(m):
        for side in range(2):
            for unit in range(len(LATE)):
                emit_side(unit, side, late_products(m, lines_total + side, unit))
        edges(LATE_ROWS)
        for unit in range(len(LATE)):
            lines = [late_products(m, e, unit) for e in range(lines_total)]
            emit_lines(unit, lines, zcbuf, LATE_STEP)

    def fresh_field(i, j, p):
        return zbuf[pl.ds(FIELDS[(i, j, p)], rows, stride=FRESH_STEP), :]

    def late_field(i, j, p):
        return zcbuf[pl.ds(LATE_FIELDS[(i, j, p)], rows, stride=LATE_STEP), :]

    class Coherence:
        def __init__(self):
            self.scales = {}
            self.slot = {}
            self.re = {}
            self.im = {}
            self.used = 0

        def keep(self, key, value):
            coh[self.used] = value
            self.slot[key] = self.used
            self.used += 1

        def get(self, key):
            return coh[self.slot[key]]

        def tally(self, sums, i, value, minus=False):
            if i in sums:
                sums[i] = sums[i] - value if minus else sums[i] + value
            else:
                sums[i] = -value if minus else value

        def add(self, images, pairs, field):
            for i in images:
                value = field(i, i, 0)
                scale = lax.rsqrt(jnp.maximum(value, covariance_floor))
                self.scales[i] = scale
                value = value * (scale * scale)
                self.keep((i, i), value)
                self.tally(self.re, i, value)
            for i, j in pairs:
                s = self.scales[i] * self.scales[j]
                c = field(i, j, 0) * s
                d = field(i, j, 1) * s
                self.keep((i, j, 0), c)
                self.keep((i, j, 1), c + d)
                self.keep((i, j, 2), c - d)
                self.tally(self.re, i, c)
                self.tally(self.re, j, c)
                self.tally(self.im, i, d)
                self.tally(self.im, j, d, True)

        def power(self):
            images = sorted(self.re)
            re = [self.re[i] for i in images]
            im = [self.im[i] for i in images]
            gain = None
            for step in range(ITERS):
                if step:
                    both = [x + y for x, y in zip(re, im)]
                    new_re, new_im = [], []
                    for i in images:
                        shared = first = second = None
                        for j in images:
                            if j == i:
                                continue
                            key = (i, j) if (i, j, 0) in self.slot else (j, i)
                            turn = key != (i, j)
                            c = self.get(key + (0,)) * both[j]
                            e = self.get(key + (2 if turn else 1,)) * im[j]
                            f = self.get(key + (1 if turn else 2,)) * re[j]
                            shared = c if shared is None else shared + c
                            first = e if first is None else first + e
                            second = f if second is None else second + f
                        c = self.get((i, i))
                        new_re.append((shared - first) + c * re[i])
                        new_im.append((shared - second) + c * im[i])
                    re, im = new_re, new_im
                squares = [x * x + y * y for x, y in zip(re, im)]
                while len(squares) > 1:
                    squares = [sum(squares[k + 1 : k + 2], squares[k]) for k in range(0, len(squares), 2)]
                length = jnp.sqrt(squares[0])
                if gain is not None:
                    length = length * gain
                inverse = 1.0 / jnp.maximum(length, 1.0)
                gain = inverse if gain is None else gain * inverse
            return length, gain, re, im

    def finish(m, number, length, gain, re, im):
        comp_re = comp_im = None
        for i in range(M):
            a = own[m, pl.ds(i, rows, stride=LINE), :]
            b = own[m, pl.ds(M + i, rows, stride=LINE), :]
            x = re[i] * a + im[i] * b
            y = re[i] * b - im[i] * a
            comp_re = x if comp_re is None else comp_re + x
            comp_im = y if comp_im is None else comp_im + y
        return comp_re * gain, comp_im * gain

    def put_linked(m, gain, re, im):
        factor = gain * mask
        for i in range(M):
            linked[m * M + i, 0] = re[i] * factor
            linked[m * M + i, 1] = im[i] * factor

    def share_of(number, length):
        share = jnp.sum(mask * length, axis=0, keepdims=True) * (1.0 / number)
        return share + pltpu.roll(share, cols // 2, 1)

    def take_fresh(m):
        each_around(lambda k: fresh_pair(m, k, False).wait_recv())
        for side, value in enumerate(gather_halo(lambda j: pack_recv[m, j])):
            halo[m, side] = value

    take_fresh(0)
    next_wave()
    fresh_fields(0)
    early = Coherence()
    early.add(range(M), PAIRS, fresh_field)
    length, gain, re, im = early.power()
    comp_re, comp_im = finish(0, M, length, gain, re, im)
    comp_send[0:rows, :] = comp_re
    comp_send[rows:, :] = comp_im
    cpack_send[...] = jnp.zeros_like(cpack_send)
    for c, value in enumerate((comp_re, comp_im)):
        for side in range(2):
            total = jnp.zeros((rows, cols), jnp.float32)
            for copy in range(3):
                turned = pltpu.roll(value, REACH * side + strip * copy, 1, stride=REACH, stride_axis=0)
                first = strip * copy + sub * REACH
                total = jnp.where((lane >= first) & (lane < first + REACH), turned, total)
            cpack_send[side, c : c + 1, :] = jnp.sum(total, axis=0, keepdims=True)

    def comp_pair(k, sending):
        dr, dc = AROUND[k]
        slot = mirror(k) if sending else k
        if dc == 0:
            source = comp_send
            target = comp_up if AROUND[slot][0] < 0 else comp_dn
        else:
            source = cpack_send.at[0 if dc < 0 else 1]
            target = cpack_recv.at[slot - 2]
        return pltpu.make_async_remote_copy(
            src_ref=source,
            dst_ref=target,
            send_sem=send_b.at[k],
            recv_sem=recv_b.at[slot],
            device_id=(my_row + dr, my_col + dc),
            device_id_type=mesh_id,
        )

    each_around(lambda k: comp_pair(k, True).start())
    next_wave()

    put_linked(0, gain, re, im)
    part[...] = share_of(M, length)
    last = MS - 1
    take_fresh(last)
    fresh_fields(last)
    joint = Coherence()
    joint.add(range(M), PAIRS, fresh_field)
    while pending:
        next_wave()

    each_around(lambda k: comp_pair(k, False).wait_recv())
    for side, value in enumerate(gather_halo(lambda j: cpack_recv[j])):
        chalo[side] = value
    late_fields(last)
    joint.add([M], LATE_PAIRS, late_field)
    length, gain, re, im = joint.power()
    lane_line = lax.broadcasted_iota(jnp.int32, (1, cols), 1)
    part[...] = jnp.where(lane_line < cols // 2, part[...], share_of(M + 1, length))

    def reduce(count, me, device, source, buffer, sends, recvs):
        copies = []
        for step in range(1, count):
            copy = pltpu.make_async_remote_copy(
                src_ref=source,
                dst_ref=buffer.at[me],
                send_sem=sends.at[step],
                recv_sem=recvs.at[me],
                device_id=device(lax.rem(me + step, count)),
                device_id_type=mesh_id,
            )
            copy.start()
            copies.append(copy)
        buffer[me] = source[...]
        for step in range(1, count):
            other = lax.rem(me + step, count)
            pltpu.make_async_remote_copy(
                src_ref=source,
                dst_ref=buffer.at[other],
                send_sem=sends.at[step],
                recv_sem=recvs.at[other],
                device_id=device(other),
                device_id_type=mesh_id,
            ).wait_recv()
        for copy in copies:
            copy.wait_send()
        total = buffer[0]
        for other in range(1, count):
            total = total + buffer[other]
        return total

    def close_last():
        comp_re, comp_im = finish(last, M + 1, length, gain, re, im)
        comp_out[0] = comp_re
        comp_out[1] = comp_im
        put_linked(last, gain, re, im)

    def flips(position, count):
        steps = []
        size = 1
        while size < count:
            steps.append(size * (1 - 2 * lax.rem(position // size, 2)))
            size *= 2
        return steps

    def swapped(position, steps, mask_bits):
        for bit, step in enumerate(steps):
            if mask_bits >> bit & 1:
                position = position + step
        return position

    if direct:
        count = row_count * col_count
        row_steps, col_steps = flips(my_row, row_count), flips(my_col, col_count)

        def weight(code):
            return -bin(code // col_count).count("1") - code % col_count

        for code in sorted(range(1, count), key=weight):
            pltpu.make_async_remote_copy(
                src_ref=part,
                dst_ref=red_row.at[code],
                send_sem=send_r.at[0],
                recv_sem=recv_r.at[0],
                device_id=(
                    swapped(my_row, row_steps, code // col_count),
                    swapped(my_col, col_steps, code % col_count),
                ),
                device_id_type=mesh_id,
            ).start()
        close_last()
        everything = pltpu.make_async_remote_copy(
            src_ref=red_row.at[pl.ds(1, count - 1)],
            dst_ref=red_row.at[pl.ds(1, count - 1)],
            send_sem=send_r.at[0],
            recv_sem=recv_r.at[0],
            device_id=(swapped(my_row, row_steps, row_count - 1), swapped(my_col, col_steps, col_count - 1)),
            device_id_type=mesh_id,
        )
        everything.wait_recv()
        values = [part[...]] + [red_row[code] for code in range(1, count)]
        while len(values) > 1:
            values = [values[k] + values[k + 1] for k in range(0, len(values), 2)]
        total = values[0]
        strength[...] = total
        everything.wait_send()
    else:
        total = reduce(row_count, my_row, lambda d: (d, my_col), part, red_row, send_r, recv_r)
        part2 = red_col.at[col_count]
        part2[...] = total
        total = reduce(col_count, my_col, lambda d: (my_row, d), part2, red_col, send_c, recv_c)
        strength[...] = total
        close_last()

    for m in range(MS):
        each_around(lambda k, m=m: fresh_pair(m, k, True).wait_send())
    each_around(lambda k: comp_pair(k, True).wait_send())


def closing(pixels, linked_in, comp_in, total, linked, comp, strength, scalars, sems):
    copies = [
        pltpu.make_async_copy(linked_in, linked, sems.at[0]),
        pltpu.make_async_copy(comp_in, comp, sems.at[1]),
        pltpu.make_async_copy(scalars, strength, sems.at[2]),
    ]
    for copy in copies[:2]:
        copy.start()
    for m in range(MS):
        lane = lax.broadcasted_iota(jnp.int32, total.shape, 1)
        mine = lane < total.shape[1] // 2 if m == 0 else lane >= total.shape[1] // 2
        scalars[m] = jnp.sum(jnp.where(mine, total[...], 0.0)) / pixels
    copies[2].start()
    for copy in copies:
        copy.wait()


def shards(slc_stack, land_mask):
    rows, cols = land_mask.shape
    row_count, col_count = lax.axis_size("row"), lax.axis_size("col")
    f32, bf16 = jnp.float32, jnp.bfloat16
    vmem = pl.BlockSpec(memory_space=pltpu.VMEM)
    dma = pltpu.SemaphoreType.DMA
    hbm = pl.BlockSpec(memory_space=pltpu.HBM)
    devices = row_count * col_count
    direct = devices <= 64 and row_count & (row_count - 1) == 0 and col_count & (col_count - 1) == 0
    peers = devices if direct else row_count
    linked_shape = jax.ShapeDtypeStruct(slc_stack.shape, f32)
    comp_shape = jax.ShapeDtypeStruct((2, rows, cols), f32)
    linked, comp, total = pl.pallas_call(
        functools.partial(kernel, row_count, col_count, direct),
        out_shape=(linked_shape, comp_shape, jax.ShapeDtypeStruct((1, cols), f32)),
        in_specs=[hbm, hbm],
        out_specs=(vmem, vmem, vmem),
        scratch_shapes=[
            pltpu.VMEM(slc_stack.shape, f32),
            pltpu.VMEM((rows, cols), jnp.int32),
            pltpu.VMEM((MS, rows * LINE + SUB, cols), f32),
            pltpu.VMEM((MS, EDGE + SUB, cols), f32),
            pltpu.VMEM((MS, EDGE + SUB, cols), f32),
            pltpu.VMEM((MS, 2, PACK, cols), f32),
            pltpu.VMEM((MS, 6, PACK, cols), f32),
            pltpu.VMEM((MS, 2, PACK, cols), f32),
            pltpu.VMEM((2 * rows, cols), f32),
            pltpu.VMEM((2 * rows, cols), f32),
            pltpu.VMEM((2 * rows, cols), f32),
            pltpu.VMEM((2, SUB, cols), f32),
            pltpu.VMEM((6, SUB, cols), f32),
            pltpu.VMEM((2, SUB, cols), f32),
            pltpu.VMEM((2 * cols, cols), bf16),
            pltpu.VMEM((2 * cols, rows * cols), bf16),
            pltpu.VMEM((len(GROUPS), rows * 2 * SUB, 2 * cols), bf16),
            pltpu.VMEM((2, FRESH_ROWS, 2 * cols), bf16),
            pltpu.VMEM((rows, FRESH_ROWS, cols), f32),
            pltpu.VMEM((rows * FRESH_STEP, cols), f32),
            pltpu.VMEM((rows * LATE_STEP, cols), f32),
            pltpu.VMEM((SLOTS, rows, cols), f32),
            pltpu.VMEM((1, cols), f32),
            pltpu.VMEM((peers, 1, cols), f32),
            pltpu.VMEM((col_count + 1, 1, cols), f32),
            dma((2,)),
            pltpu.SemaphoreType.REGULAR((max(1, len(waves(row_count, col_count))),)),
            dma((MS, len(AROUND))),
            dma((MS, len(AROUND))),
            dma((len(AROUND),)),
            dma((len(AROUND),)),
            dma((peers,)),
            dma((peers,)),
            dma((col_count,)),
            dma((col_count,)),
        ],
        compiler_params=pltpu.CompilerParams(collective_id=0, has_side_effects=True, vmem_limit_bytes=16 << 20),
        name="linker",
    )(*(pltpu.with_memory_space_constraint(x, pltpu.HBM) for x in (slc_stack, land_mask)))
    return pl.pallas_call(
        functools.partial(closing, rows * cols * devices),
        out_shape=(linked_shape, comp_shape, jax.ShapeDtypeStruct((MS,), f32)),
        in_specs=[vmem, vmem, vmem],
        out_specs=(hbm, hbm, hbm),
        scratch_shapes=[pltpu.SMEM((MS,), f32), dma((3,))],
        compiler_params=pltpu.CompilerParams(vmem_limit_bytes=4 << 20),
        name="closing",
    )(linked, comp, total)


def solution(mesh):
    return jax.shard_map(
        shards,
        mesh=mesh,
        in_specs=(P(None, None, "row", "col"), P("row", "col")),
        out_specs=(P(None, None, "row", "col"), P(None, "row", "col"), P()),
        check_vma=False,
    )
```

time: 24 us -> 21.3 us (0.89)
  Pallas kernels: 23.2 us -> 20.5 us
    pallas_call x1, Pallas kernels: 22 us -> 19.8 us  [shards(): pl.pallas_call(functools.partial(kernel, row_count, col_count, direct), o...]
    pallas_call x1, Pallas kernels: 1.2 us -> 0.71 us  [shards(): pl.pallas_call(functools.partial(closing, rows * cols * devices), out_sha...]
where the time goes in v1:
time: 21.3 us; the launch traced here: 21.2 us
  Pallas kernels  20.5 us (96%)
  between operations  0.64 us (3%)
    pallas_call x1, Pallas kernels, shards(): pl.pallas_call(functools.partial(kernel, row_count, col_count, direct), o...  19.8 us
    pallas_call x1, Pallas kernels, shards(): pl.pallas_call(functools.partial(closing, rows * cols * devices), out_sha...  0.71 us

profile of v1, /device:TPU:0, one launch (start us, length us, event | category | flops | bytes accessed | tf_op | source)
XLA Modules:
  0.0 21.2 jit_solution(18025356584012452262)
XLA Ops:
  0.6 19.8 %linker.1 = (f32[20,2,8,128]{3,2,1,0:T(8,128)S(1)}, f32[2,8,128]{2,1,0:T(8,128)S(1)}, f32[1,128]{1,0:T(1,128)S(1)}) custom-call(f32[20,2,8,128]{3,2,1,0:T(8,128)} %slc_hbm.1, s32[8,128]{1,0:T(8,128)} %land_hbm.1), custom_call_target="tpu_custom_call" | custom-call | tf_op jit(solution)/shard_map/linker/pallas_call | solution.py:723
  20.5 0.7 %closing.1 = (f32[20,2,8,128]{3,2,1,0:T(8,128)}, f32[2,8,128]{2,1,0:T(8,128)}, f32[2]{0:T(128)}) custom-call(f32[20,2,8,128]{3,2,1,0:T(8,128)S(1)} %get-tuple-element.6.linked_in, f32[2,8,128]{2,1,0:T(8,128)S(1)} %get-tuple-element.7.comp_in, f32[1,128]{1,0:T(1,128)S(1)} %get-tuple-element.8.total), custom_call_target="tpu_custom_call" | custom-call | tf_op jit(solution)/shard_map/closing/pallas_call | solution.py:768

commit v2 on v1

--- a/solution.py
+++ b/solution.py
@@ -24,12 +24,11 @@
 
 
 def pair_groups():
-    groups = [[(s, (s + lag) % SUB) for s in range(SUB)] for lag in range(1, SUB // 2)]
+    groups = [[(s, (s + lag) % SUB) for s in range(SUB)] for lag in range(SUB // 2)]
     half = SUB // 2
     groups.append([(s, s + half) for s in range(half)] + [(M - 2, M - 1), (M - 2, M - 2), (M - 1, M - 1)])
     groups.append([(s, M - 2) for s in range(SUB)])
     groups.append([(s, M - 1) for s in range(SUB)])
-    groups.append([(s, s) for s in range(SUB)])
     return groups
 
 
@@ -55,20 +54,43 @@
 SLOTS = 3 * (len(PAIRS) + len(LATE_PAIRS)) + M + 1
 
 
-def window_sums(lines, outputs):
-    core = lines[outputs - 1]
-    for e in range(outputs, WIN):
-        core = core + lines[e]
-    low = [None] * outputs
-    low[outputs - 1] = core
-    for r in range(outputs - 2, -1, -1):
-        low[r] = low[r + 1] + lines[r]
-    sums = [low[0]]
-    high = None
-    for r in range(1, outputs):
-        extra = lines[WIN - 1 + r]
-        high = extra if high is None else high + extra
-        sums.append(low[r] + high)
+def own_range(r, rows):
+    return max(r, REACH), min(r + WIN, REACH + rows)
+
+
+def own_sums(lines, rows):
+    core = lines[rows - 1 - REACH]
+    for e in range(rows, WIN):
+        core = core + lines[e - REACH]
+    starts = {rows - 1: core}
+    for e in range(rows - 2, REACH - 1, -1):
+        starts[e] = starts[e + 1] + lines[e - REACH]
+    tails = {WIN: None}
+    for e in range(WIN, REACH + rows):
+        tails[e + 1] = lines[e - REACH] if tails[e] is None else tails[e] + lines[e - REACH]
+    sums = {}
+    for r in range(rows):
+        start, stop = own_range(r, rows)
+        if (start, stop) not in sums:
+            tail = tails[stop]
+            sums[(start, stop)] = starts[start] if tail is None else starts[start] + tail
+    return sums
+
+
+def window_sums(above, below, partial, rows):
+    lead = {REACH: None}
+    for e in range(REACH - 1, -1, -1):
+        lead[e] = above[e] if lead[e + 1] is None else lead[e + 1] + above[e]
+    trail = {0: None}
+    for e in range(REACH):
+        trail[e + 1] = below[e] if trail[e] is None else trail[e] + below[e]
+    sums = []
+    for r in range(rows):
+        total = partial(r)
+        for extra in (lead[min(r, REACH)], trail[max(0, r + WIN - REACH - rows)]):
+            if extra is not None:
+                total = total + extra
+        sums.append(total)
     return sums
 
 
@@ -112,6 +134,7 @@
     chalo,
     w_main,
     w_halo,
+    pbuf,
     ybuf,
     hbuf,
     ebuf,
@@ -129,8 +152,6 @@
     recv_b,
     send_r,
     recv_r,
-    send_c,
-    recv_c,
 ):
     rows, cols = land.shape
     my_row = lax.axis_index("row")
@@ -138,8 +159,9 @@
     strip = rows * REACH
     mesh_id = pl.DeviceIdType.MESH
     loads = [
-        pltpu.make_async_copy(slc_hbm, slc, load_sem.at[0]),
-        pltpu.make_async_copy(land_hbm, land, load_sem.at[1]),
+        pltpu.make_async_copy(land_hbm, land, load_sem.at[MS]),
+    ] + [
+        pltpu.make_async_copy(slc_hbm.at[pl.ds(m * M, M)], slc.at[pl.ds(m * M, M)], load_sem.at[m]) for m in range(MS)
     ]
     for load in loads:
         load.start()
@@ -205,7 +227,7 @@
     lane = lax.broadcasted_iota(jnp.int32, (rows, cols), 1)
     sub = lax.broadcasted_iota(jnp.int32, (rows, cols), 0)
 
-    for load in loads:
+    for load in loads[:2]:
         load.wait()
     mask = land[...].astype(jnp.float32)
 
@@ -250,28 +272,31 @@
         return pltpu.make_async_remote_copy(
             src_ref=source,
             dst_ref=target,
-            send_sem=send_a.at[m, k],
+            send_sem=send_a.at[k],
             recv_sem=recv_a.at[m, slot],
             device_id=(my_row + dr, my_col + dc),
             device_id_type=mesh_id,
         )
 
-    def each_around(action):
-        for k in range(len(AROUND)):
+    def each_around(action, which=range(len(AROUND))):
+        for k in which:
 
             @pl.when(exists[k])
             def _(k=k):
                 action(k)
 
+    beside, strips = range(2), range(2, len(AROUND))
     place(0)
+    pl.semaphore_wait(barrier, expected)
+    each_around(lambda k: fresh_pair(0, k, True).start(), beside)
     pack(0)
-    pl.semaphore_wait(barrier, expected)
-    each_around(lambda k: fresh_pair(0, k, True).start())
+    each_around(lambda k: fresh_pair(0, k, True).start(), strips)
+    next_wave()
     for m in range(1, MS):
+        loads[1 + m].wait()
         place(m)
         pack(m)
         each_around(lambda k, m=m: fresh_pair(m, k, True).start())
-    next_wave()
 
     k_at = lax.broadcasted_iota(jnp.int32, (cols, cols), 0)
     n_at = lax.broadcasted_iota(jnp.int32, (cols, cols), 1)
@@ -321,9 +346,11 @@
 
     def operands(tile, unit):
         lead = [tile(c, 0) for c in range(2)]
-        if unit < SUB // 2 - 1:
-            return lead, [pltpu.roll(v, SUB - 1 - unit, 0) for v in lead]
-        if unit == SUB // 2 - 1:
+        if unit == 0:
+            return lead, lead
+        if unit < SUB // 2:
+            return lead, [pltpu.roll(v, SUB - unit, 0) for v in lead]
+        if unit == SUB // 2:
             left, right = [], []
             for c in range(2):
                 mid, late = tile(c, SUB // 2), tile(c, SUB - M + 5)
@@ -334,10 +361,10 @@
 
     def products(tile, row_tile, unit):
         (a, b), other = operands(tile, unit)
-        if unit == len(GROUPS) - 1:
+        if unit == 0:
             return a * a + b * b, None
         if other is None:
-            image = M - 2 + unit - SUB // 2
+            image = M - 3 + unit - SUB // 2
             x, y = (jnp.broadcast_to(row_tile(c, image), (SUB, cols)) for c in range(2))
         else:
             x, y = other
@@ -367,8 +394,21 @@
             ebuf[r, 0:count] = value[:, 0:cols]
             ebuf[r + 1, 0:count] = value[:, cols:]
 
+    partials = {}
+    for r in range(rows):
+        partials.setdefault(own_range(r, rows), len(partials))
+
+    def keep_own(unit, lines):
+        for key, value in own_sums(lines, rows).items():
+            at = (unit * len(partials) + partials[key]) * 2 * SUB
+            pbuf[at : at + 2 * SUB, :] = value
+
     def emit_lines(unit, lines, target, step):
-        for r, total in enumerate(window_sums(lines, rows)):
+        def partial(r):
+            at = (unit * len(partials) + partials[own_range(r, rows)]) * 2 * SUB
+            return pbuf[at : at + 2 * SUB, :]
+
+        for r, total in enumerate(window_sums(lines[:REACH], lines[REACH:], partial, rows)):
             high, low = split(total)
             ybuf[unit, r * 2 * SUB : (r + 1) * 2 * SUB, 0:cols] = high
             ybuf[unit, r * 2 * SUB : (r + 1) * 2 * SUB, cols:] = low
@@ -383,15 +423,25 @@
         first, second = pair
         return jnp.concatenate([first, jnp.zeros_like(first) if second is None else second], 0)
 
-    def fresh_fields(m):
+    own_lines = range(REACH, REACH + rows)
+    far_lines = [*range(REACH), *range(REACH + rows, lines_total)]
+
+    def fresh_values(m, e, unit):
+        return both_halves(products(tile_of(m, e), row_of(m, e), unit))
+
+    def fresh_own(m):
+        for unit in range(len(GROUPS)):
+            keep_own(unit, [fresh_values(m, e, unit) for e in own_lines])
+
+    def fresh_sides(m):
         for side in range(2):
             for unit in range(len(GROUPS)):
-                e = lines_total + side
-                emit_side(unit, side, both_halves(products(tile_of(m, e), row_of(m, e), unit)))
+                emit_side(unit, side, fresh_values(m, lines_total + side, unit))
         edges(FRESH_ROWS)
+
+    def fresh_far(m):
         for unit in range(len(GROUPS)):
-            lines = [both_halves(products(tile_of(m, e), row_of(m, e), unit)) for e in range(lines_total)]
-            emit_lines(unit, lines, zbuf, FRESH_STEP)
+            emit_lines(unit, [fresh_values(m, e, unit) for e in far_lines], zbuf, FRESH_STEP)
 
     def comp_row(e, c):
         if e < REACH:
@@ -420,8 +470,11 @@
                 emit_side(unit, side, late_products(m, lines_total + side, unit))
         edges(LATE_ROWS)
         for unit in range(len(LATE)):
-            lines = [late_products(m, e, unit) for e in range(lines_total)]
-            emit_lines(unit, lines, zcbuf, LATE_STEP)
+            emit_lines(unit, [late_products(m, e, unit) for e in far_lines], zcbuf, LATE_STEP)
+
+    def late_own(m):
+        for unit in range(len(LATE)):
+            keep_own(unit, [late_products(m, e, unit) for e in own_lines])
 
     def fresh_field(i, j, p):
         return zbuf[pl.ds(FIELDS[(i, j, p)], rows, stride=FRESH_STEP), :]
@@ -525,32 +578,28 @@
             linked[m * M + i, 1] = im[i] * factor
 
     def share_of(number, length):
-        share = jnp.sum(mask * length, axis=0, keepdims=True) * (1.0 / number)
-        return share + pltpu.roll(share, cols // 2, 1)
-
-    def take_fresh(m):
-        each_around(lambda k: fresh_pair(m, k, False).wait_recv())
+        return jnp.sum(mask * length, axis=0, keepdims=True) * (1.0 / number)
+
+    def take_strips(m):
+        each_around(lambda k: fresh_pair(m, k, False).wait_recv(), strips)
         for side, value in enumerate(gather_halo(lambda j: pack_recv[m, j])):
             halo[m, side] = value
 
-    take_fresh(0)
+    def take_beside(m):
+        each_around(lambda k: fresh_pair(m, k, False).wait_recv(), beside)
+
+    fresh_own(0)
+    take_strips(0)
+    fresh_sides(0)
     next_wave()
-    fresh_fields(0)
+    take_beside(0)
+    fresh_far(0)
     early = Coherence()
     early.add(range(M), PAIRS, fresh_field)
     length, gain, re, im = early.power()
     comp_re, comp_im = finish(0, M, length, gain, re, im)
     comp_send[0:rows, :] = comp_re
     comp_send[rows:, :] = comp_im
-    cpack_send[...] = jnp.zeros_like(cpack_send)
-    for c, value in enumerate((comp_re, comp_im)):
-        for side in range(2):
-            total = jnp.zeros((rows, cols), jnp.float32)
-            for copy in range(3):
-                turned = pltpu.roll(value, REACH * side + strip * copy, 1, stride=REACH, stride_axis=0)
-                first = strip * copy + sub * REACH
-                total = jnp.where((lane >= first) & (lane < first + REACH), turned, total)
-            cpack_send[side, c : c + 1, :] = jnp.sum(total, axis=0, keepdims=True)
 
     def comp_pair(k, sending):
         dr, dc = AROUND[k]
@@ -570,17 +619,31 @@
             device_id_type=mesh_id,
         )
 
-    each_around(lambda k: comp_pair(k, True).start())
-    next_wave()
+    each_around(lambda k: comp_pair(k, True).start(), beside)
+    cpack_send[...] = jnp.zeros_like(cpack_send)
+    for c, value in enumerate((comp_re, comp_im)):
+        for side in range(2):
+            total = jnp.zeros((rows, cols), jnp.float32)
+            for copy in range(3):
+                turned = pltpu.roll(value, REACH * side + strip * copy, 1, stride=REACH, stride_axis=0)
+                first = strip * copy + sub * REACH
+                total = jnp.where((lane >= first) & (lane < first + REACH), turned, total)
+            cpack_send[side, c : c + 1, :] = jnp.sum(total, axis=0, keepdims=True)
+
+    each_around(lambda k: comp_pair(k, True).start(), (2, 4, 5, 7, 3, 6))
 
     put_linked(0, gain, re, im)
-    part[...] = share_of(M, length)
+    part[0:1] = share_of(M, length)
     last = MS - 1
-    take_fresh(last)
-    fresh_fields(last)
+    fresh_own(last)
+    take_strips(last)
+    fresh_sides(last)
+    take_beside(last)
+    fresh_far(last)
+    late_own(last)
     joint = Coherence()
     joint.add(range(M), PAIRS, fresh_field)
-    while pending:
+    while len(pending) and pending[0][0] < len(offsets) - 1:
         next_wave()
 
     each_around(lambda k: comp_pair(k, False).wait_recv())
@@ -589,8 +652,9 @@
     late_fields(last)
     joint.add([M], LATE_PAIRS, late_field)
     length, gain, re, im = joint.power()
-    lane_line = lax.broadcasted_iota(jnp.int32, (1, cols), 1)
-    part[...] = jnp.where(lane_line < cols // 2, part[...], share_of(M + 1, length))
+    part[last : last + 1] = share_of(M + 1, length)
+    while pending:
+        next_wave()
 
     def reduce(count, me, device, source, buffer, sends, recvs):
         copies = []
@@ -629,6 +693,25 @@
         comp_out[1] = comp_im
         put_linked(last, gain, re, im)
 
+    def sent(k):
+        dr, dc = AROUND[k]
+        if dc == 0:
+            source, target = own.at[:, pl.ds(0, EDGE)], up.at[:, pl.ds(0, EDGE)]
+        else:
+            source, target = pack_send.at[:, 0], pack_recv.at[:, 0]
+        return pltpu.make_async_remote_copy(
+            src_ref=source,
+            dst_ref=target,
+            send_sem=send_a.at[k],
+            recv_sem=recv_a.at[0, k],
+            device_id=(my_row + dr, my_col + dc),
+            device_id_type=mesh_id,
+        )
+
+    def finish_sends():
+        each_around(lambda k: sent(k).wait_send())
+        each_around(lambda k: comp_pair(k, True).wait_send())
+
     def flips(position, count):
         steps = []
         size = 1
@@ -663,6 +746,7 @@
                 device_id_type=mesh_id,
             ).start()
         close_last()
+        finish_sends()
         everything = pltpu.make_async_remote_copy(
             src_ref=red_row.at[pl.ds(1, count - 1)],
             dst_ref=red_row.at[pl.ds(1, count - 1)],
@@ -682,13 +766,10 @@
         total = reduce(row_count, my_row, lambda d: (d, my_col), part, red_row, send_r, recv_r)
         part2 = red_col.at[col_count]
         part2[...] = total
-        total = reduce(col_count, my_col, lambda d: (my_row, d), part2, red_col, send_c, recv_c)
+        total = reduce(col_count, my_col, lambda d: (my_row, d), part2, red_col, send_r.at[pl.ds(row_count, col_count)], recv_r.at[pl.ds(row_count, col_count)])
         strength[...] = total
         close_last()
-
-    for m in range(MS):
-        each_around(lambda k, m=m: fresh_pair(m, k, True).wait_send())
-    each_around(lambda k: comp_pair(k, True).wait_send())
+        finish_sends()
 
 
 def closing(pixels, linked_in, comp_in, total, linked, comp, strength, scalars, sems):
@@ -700,9 +781,7 @@
     for copy in copies[:2]:
         copy.start()
     for m in range(MS):
-        lane = lax.broadcasted_iota(jnp.int32, total.shape, 1)
-        mine = lane < total.shape[1] // 2 if m == 0 else lane >= total.shape[1] // 2
-        scalars[m] = jnp.sum(jnp.where(mine, total[...], 0.0)) / pixels
+        scalars[m] = jnp.sum(total[m : m + 1]) / pixels
     copies[2].start()
     for copy in copies:
         copy.wait()
@@ -722,7 +801,7 @@
     comp_shape = jax.ShapeDtypeStruct((2, rows, cols), f32)
     linked, comp, total = pl.pallas_call(
         functools.partial(kernel, row_count, col_count, direct),
-        out_shape=(linked_shape, comp_shape, jax.ShapeDtypeStruct((1, cols), f32)),
+        out_shape=(linked_shape, comp_shape, jax.ShapeDtypeStruct((MS, cols), f32)),
         in_specs=[hbm, hbm],
         out_specs=(vmem, vmem, vmem),
         scratch_shapes=[
@@ -742,25 +821,24 @@
             pltpu.VMEM((2, SUB, cols), f32),
             pltpu.VMEM((2 * cols, cols), bf16),
             pltpu.VMEM((2 * cols, rows * cols), bf16),
+            pltpu.VMEM((len(GROUPS) * rows * 2 * SUB, cols), f32),
             pltpu.VMEM((len(GROUPS), rows * 2 * SUB, 2 * cols), bf16),
             pltpu.VMEM((2, FRESH_ROWS, 2 * cols), bf16),
             pltpu.VMEM((rows, FRESH_ROWS, cols), f32),
             pltpu.VMEM((rows * FRESH_STEP, cols), f32),
             pltpu.VMEM((rows * LATE_STEP, cols), f32),
             pltpu.VMEM((SLOTS, rows, cols), f32),
-            pltpu.VMEM((1, cols), f32),
-            pltpu.VMEM((peers, 1, cols), f32),
-            pltpu.VMEM((col_count + 1, 1, cols), f32),
-            dma((2,)),
+            pltpu.VMEM((MS, cols), f32),
+            pltpu.VMEM((peers, MS, cols), f32),
+            pltpu.VMEM((col_count + 1, MS, cols), f32),
+            dma((MS + 1,)),
             pltpu.SemaphoreType.REGULAR((max(1, len(waves(row_count, col_count))),)),
-            dma((MS, len(AROUND))),
+            dma((len(AROUND),)),
             dma((MS, len(AROUND))),
             dma((len(AROUND),)),
             dma((len(AROUND),)),
-            dma((peers,)),
-            dma((peers,)),
-            dma((col_count,)),
-            dma((col_count,)),
+            dma((1 if direct else row_count + col_count,)),
+            dma((1 if direct else row_count + col_count,)),
         ],
         compiler_params=pltpu.CompilerParams(collective_id=0, has_side_effects=True, vmem_limit_bytes=16 << 20),
         name="linker",

time: 21.3 us -> 20.4 us (0.958)
  Pallas kernels: 20.5 us -> 19.5 us
    pallas_call x1, Pallas kernels: 19.8 us -> 18.8 us  [shards(): pl.pallas_call(functools.partial(kernel, row_count, col_count, direct), o...]
where the time goes in v2:
time: 20.4 us; the launch traced here: 20.2 us
  Pallas kernels  19.5 us (96%)
  between operations  0.64 us (3%)
    pallas_call x1, Pallas kernels, shards(): pl.pallas_call(functools.partial(kernel, row_count, col_count, direct), o...  18.8 us
    pallas_call x1, Pallas kernels, shards(): pl.pallas_call(functools.partial(closing, rows * cols * devices), out_sha...  0.71 us

profile of v2, /device:TPU:0, one launch (start us, length us, event | category | flops | bytes accessed | tf_op | source)
XLA Modules:
  0.0 20.2 jit_solution(3084590629440878171)
XLA Ops:
  0.6 18.8 %linker.1 = (f32[20,2,8,128]{3,2,1,0:T(8,128)S(1)}, f32[2,8,128]{2,1,0:T(8,128)S(1)}, f32[2,128]{1,0:T(2,128)S(1)}) custom-call(f32[20,2,8,128]{3,2,1,0:T(8,128)} %slc_hbm.1, s32[8,128]{1,0:T(8,128)} %land_hbm.1), custom_call_target="tpu_custom_call" | custom-call | tf_op jit(solution)/shard_map/linker/pallas_call | solution.py:802
  19.5 0.7 %closing.1 = (f32[20,2,8,128]{3,2,1,0:T(8,128)}, f32[2,8,128]{2,1,0:T(8,128)}, f32[2]{0:T(128)}) custom-call(f32[20,2,8,128]{3,2,1,0:T(8,128)S(1)} %get-tuple-element.6.linked_in, f32[2,8,128]{2,1,0:T(8,128)S(1)} %get-tuple-element.7.comp_in, f32[2,128]{1,0:T(2,128)S(1)} %get-tuple-element.8.total), custom_call_target="tpu_custom_call" | custom-call | tf_op jit(solution)/shard_map/closing/pallas_call | solution.py:846

commit v3 on v2

--- a/solution.py
+++ b/solution.py
@@ -237,23 +237,22 @@
                 own[m, pl.ds(c * M + i, rows, stride=LINE), :] = slc[m * M + i, c] * mask
         own[m, rows * LINE :, :] = jnp.zeros((own.shape[1] - rows * LINE, cols), jnp.float32)
 
-    def spread(line, shift):
-        total = pltpu.roll(line, cols - shift, 1) if shift else line
-        return (
-            total
-            + pltpu.roll(line, (strip - shift) % cols, 1)
-            + pltpu.roll(line, (2 * strip - shift) % cols, 1)
-        )
-
     def pack(m):
-        for at in range(0, PACK, SUB):
+        packed = [jnp.zeros((SUB, cols), jnp.float32)] * 2
+        for block in range(PACK // SUB):
+            at = block * SUB
             low = high = jnp.zeros((SUB, cols), jnp.float32)
             for r in range(rows):
                 turned = pltpu.roll(own[m, r * LINE + at : r * LINE + at + SUB, :], REACH * (r + 1), 1)
                 high = jnp.where((lane >= r * REACH) & (lane < (r + 1) * REACH), turned, high)
                 low = jnp.where((lane >= (r + 1) * REACH) & (lane < (r + 2) * REACH), turned, low)
-            pack_send[m, 0, at : at + SUB, :] = spread(low, REACH)
-            pack_send[m, 1, at : at + SUB, :] = spread(high, 0)
+            here = (lane >= block * strip) & (lane < (block + 1) * strip)
+            for side, value in enumerate((pltpu.roll(low, (block * strip - REACH) % cols, 1), high)):
+                if side and block:
+                    value = pltpu.roll(value, block * strip, 1)
+                packed[side] = jnp.where(here, value, packed[side])
+        for side in range(2):
+            pack_send[m, side] = packed[side]
 
     def mirror(k):
         dr, dc = AROUND[k]
@@ -286,17 +285,12 @@
                 action(k)
 
     beside, strips = range(2), range(2, len(AROUND))
+    outward = (2, 4, 5, 7, 3, 6, 0, 1)
     place(0)
+    pack(0)
     pl.semaphore_wait(barrier, expected)
-    each_around(lambda k: fresh_pair(0, k, True).start(), beside)
-    pack(0)
-    each_around(lambda k: fresh_pair(0, k, True).start(), strips)
+    each_around(lambda k: fresh_pair(0, k, True).start(), outward)
     next_wave()
-    for m in range(1, MS):
-        loads[1 + m].wait()
-        place(m)
-        pack(m)
-        each_around(lambda k, m=m: fresh_pair(m, k, True).start())
 
     k_at = lax.broadcasted_iota(jnp.int32, (cols, cols), 0)
     n_at = lax.broadcasted_iota(jnp.int32, (cols, cols), 1)
@@ -582,14 +576,27 @@
 
     def take_strips(m):
         each_around(lambda k: fresh_pair(m, k, False).wait_recv(), strips)
-        for side, value in enumerate(gather_halo(lambda j: pack_recv[m, j])):
-            halo[m, side] = value
+        for block in range(PACK // SUB):
+
+            def turned(j, block=block):
+                value = pack_recv[m, j]
+                shift = (j % 3 - block) * strip % cols
+                return pltpu.roll(value, shift, 1) if shift else value
+
+            for side, value in enumerate(gather_halo(turned)):
+                halo[m, side, block * SUB : (block + 1) * SUB, :] = value
 
     def take_beside(m):
         each_around(lambda k: fresh_pair(m, k, False).wait_recv(), beside)
 
     fresh_own(0)
+    for m in range(1, MS):
+        loads[1 + m].wait()
+        place(m)
+        pack(m)
     take_strips(0)
+    for m in range(1, MS):
+        each_around(lambda k, m=m: fresh_pair(m, k, True).start(), outward)
     fresh_sides(0)
     next_wave()
     take_beside(0)
@@ -620,7 +627,6 @@
         )
 
     each_around(lambda k: comp_pair(k, True).start(), beside)
-    cpack_send[...] = jnp.zeros_like(cpack_send)
     for c, value in enumerate((comp_re, comp_im)):
         for side in range(2):
             total = jnp.zeros((rows, cols), jnp.float32)
@@ -810,15 +816,15 @@
             pltpu.VMEM((MS, rows * LINE + SUB, cols), f32),
             pltpu.VMEM((MS, EDGE + SUB, cols), f32),
             pltpu.VMEM((MS, EDGE + SUB, cols), f32),
-            pltpu.VMEM((MS, 2, PACK, cols), f32),
-            pltpu.VMEM((MS, 6, PACK, cols), f32),
+            pltpu.VMEM((MS, 2, SUB, cols), f32),
+            pltpu.VMEM((MS, 6, SUB, cols), f32),
             pltpu.VMEM((MS, 2, PACK, cols), f32),
             pltpu.VMEM((2 * rows, cols), f32),
             pltpu.VMEM((2 * rows, cols), f32),
             pltpu.VMEM((2 * rows, cols), f32),
-            pltpu.VMEM((2, SUB, cols), f32),
-            pltpu.VMEM((6, SUB, cols), f32),
-            pltpu.VMEM((2, SUB, cols), f32),
+            pltpu.VMEM((2, 2, cols), f32),
+            pltpu.VMEM((6, 2, cols), f32),
+            pltpu.VMEM((2, 2, cols), f32),
             pltpu.VMEM((2 * cols, cols), bf16),
             pltpu.VMEM((2 * cols, rows * cols), bf16),
             pltpu.VMEM((len(GROUPS) * rows * 2 * SUB, cols), f32),

time: 20.4 us -> 19.4 us (0.951)
  Pallas kernels: 19.5 us -> 18.5 us
    pallas_call x1, Pallas kernels: 18.8 us -> 17.8 us  [shards(): pl.pallas_call(functools.partial(kernel, row_count, col_count, direct), o...]
where the time goes in v3:
time: 19.4 us; the launch traced here: 19.2 us
  Pallas kernels  18.5 us (95%)
  between operations  0.64 us (3%)
    pallas_call x1, Pallas kernels, shards(): pl.pallas_call(functools.partial(kernel, row_count, col_count, direct), o...  17.8 us
    pallas_call x1, Pallas kernels, shards(): pl.pallas_call(functools.partial(closing, rows * cols * devices), out_sha...  0.71 us

profile of v3, /device:TPU:0, one launch (start us, length us, event | category | flops | bytes accessed | tf_op | source)
XLA Modules:
  0.0 19.2 jit_solution(6356945727603102744)
XLA Ops:
  0.6 17.8 %linker.1 = (f32[20,2,8,128]{3,2,1,0:T(8,128)S(1)}, f32[2,8,128]{2,1,0:T(8,128)S(1)}, f32[2,128]{1,0:T(2,128)S(1)}) custom-call(f32[20,2,8,128]{3,2,1,0:T(8,128)} %slc_hbm.1, s32[8,128]{1,0:T(8,128)} %land_hbm.1), custom_call_target="tpu_custom_call" | custom-call | tf_op jit(solution)/shard_map/linker/pallas_call | solution.py:808
  18.5 0.7 %closing.1 = (f32[20,2,8,128]{3,2,1,0:T(8,128)}, f32[2,8,128]{2,1,0:T(8,128)}, f32[2]{0:T(128)}) custom-call(f32[20,2,8,128]{3,2,1,0:T(8,128)S(1)} %get-tuple-element.6.linked_in, f32[2,8,128]{2,1,0:T(8,128)S(1)} %get-tuple-element.7.comp_in, f32[2,128]{1,0:T(2,128)S(1)} %get-tuple-element.8.total), custom_call_target="tpu_custom_call" | custom-call | tf_op jit(solution)/shard_map/closing/pallas_call | solution.py:852

commit v4 on v3

--- a/solution.py
+++ b/solution.py
@@ -178,7 +178,7 @@
 
     def greet(semaphore, far):
         expected = jnp.int32(0)
-        for k, (dr, dc) in enumerate(AROUND):
+        for dr, dc in sorted(AROUND, key=lambda step: -abs(step[0]) - abs(step[1])):
             if (dr and far >= row_count) or (dc and far >= col_count):
                 continue
             there = existing(dr, dc, far)
@@ -373,18 +373,17 @@
         tile = tile_of(m, e)
         return lambda c, image: tile(c, image)[0:1]
 
-    def emit_side(unit, side, value):
+    def emit_side(unit, side, value, count):
         high, low = split(value)
-        at = slice(unit * 2 * SUB, (unit + 1) * 2 * SUB)
-        hbuf[0, at, side * cols : (side + 1) * cols] = high
-        hbuf[1, at, side * cols : (side + 1) * cols] = low
+        at = unit * 2 * SUB
+        hbuf[at : at + 2 * SUB, side * cols : (side + 1) * cols] = high
+        hbuf[count + at : count + at + 2 * SUB, side * cols : (side + 1) * cols] = low
 
     def edges(count):
         for r in range(0, rows, 2):
             band = w_halo[:, r * cols : (r + 2) * cols]
-            value = jnp.dot(hbuf[0, 0:count], band, preferred_element_type=jnp.float32) + jnp.dot(
-                hbuf[1, 0:count], band, preferred_element_type=jnp.float32
-            )
+            value = jnp.dot(hbuf[0 : 2 * count], band, preferred_element_type=jnp.float32)
+            value = value[0:count] + value[count:]
             ebuf[r, 0:count] = value[:, 0:cols]
             ebuf[r + 1, 0:count] = value[:, cols:]
 
@@ -397,7 +396,7 @@
             at = (unit * len(partials) + partials[key]) * 2 * SUB
             pbuf[at : at + 2 * SUB, :] = value
 
-    def emit_lines(unit, lines, target, step):
+    def emit_lines(unit, lines):
         def partial(r):
             at = (unit * len(partials) + partials[own_range(r, rows)]) * 2 * SUB
             return pbuf[at : at + 2 * SUB, :]
@@ -406,7 +405,8 @@
             high, low = split(total)
             ybuf[unit, r * 2 * SUB : (r + 1) * 2 * SUB, 0:cols] = high
             ybuf[unit, r * 2 * SUB : (r + 1) * 2 * SUB, cols:] = low
-        main = jnp.dot(ybuf[unit], w_main[...], preferred_element_type=jnp.float32)
+
+    def emit_main(unit, main, target, step):
         for r in range(rows):
             at = r * step + unit * 2 * SUB
             target[at : at + 2 * SUB, :] = (
@@ -430,12 +430,14 @@
     def fresh_sides(m):
         for side in range(2):
             for unit in range(len(GROUPS)):
-                emit_side(unit, side, fresh_values(m, lines_total + side, unit))
+                emit_side(unit, side, fresh_values(m, lines_total + side, unit), FRESH_ROWS)
         edges(FRESH_ROWS)
 
     def fresh_far(m):
         for unit in range(len(GROUPS)):
-            emit_lines(unit, [fresh_values(m, e, unit) for e in far_lines], zbuf, FRESH_STEP)
+            emit_lines(unit, [fresh_values(m, e, unit) for e in far_lines])
+            main = jnp.dot(ybuf[unit], w_main[...], preferred_element_type=jnp.float32)
+            emit_main(unit, main, zbuf, FRESH_STEP)
 
     def comp_row(e, c):
         if e < REACH:
@@ -461,10 +463,16 @@
     def late_fields(m):
         for side in range(2):
             for unit in range(len(LATE)):
-                emit_side(unit, side, late_products(m, lines_total + side, unit))
+                emit_side(unit, side, late_products(m, lines_total + side, unit), LATE_ROWS)
         edges(LATE_ROWS)
         for unit in range(len(LATE)):
-            emit_lines(unit, [late_products(m, e, unit) for e in far_lines], zcbuf, LATE_STEP)
+            emit_lines(unit, [late_products(m, e, unit) for e in far_lines])
+        size = rows * 2 * SUB
+        main = jnp.dot(
+            ybuf[0 : len(LATE)].reshape(len(LATE) * size, 2 * cols), w_main[...], preferred_element_type=jnp.float32
+        )
+        for unit in range(len(LATE)):
+            emit_main(unit, main[unit * size : (unit + 1) * size], zcbuf, LATE_STEP)
 
     def late_own(m):
         for unit in range(len(LATE)):
@@ -829,7 +837,7 @@
             pltpu.VMEM((2 * cols, rows * cols), bf16),
             pltpu.VMEM((len(GROUPS) * rows * 2 * SUB, cols), f32),
             pltpu.VMEM((len(GROUPS), rows * 2 * SUB, 2 * cols), bf16),
-            pltpu.VMEM((2, FRESH_ROWS, 2 * cols), bf16),
+            pltpu.VMEM((2 * FRESH_ROWS, 2 * cols), bf16),
             pltpu.VMEM((rows, FRESH_ROWS, cols), f32),
             pltpu.VMEM((rows * FRESH_STEP, cols), f32),
             pltpu.VMEM((rows * LATE_STEP, cols), f32),

time: 19.4 us -> 19.3 us (level)
  no operation moved by 1% of the time
where the time goes in v4:
time: 19.3 us; the launch traced here: 19.1 us
  Pallas kernels  18.4 us (95%)
  between operations  0.64 us (3%)
    pallas_call x1, Pallas kernels, shards(): pl.pallas_call(functools.partial(kernel, row_count, col_count, direct), o...  17.7 us
    pallas_call x1, Pallas kernels, shards(): pl.pallas_call(functools.partial(closing, rows * cols * devices), out_sha...  0.71 us

profile of v4, /device:TPU:0, one launch (start us, length us, event | category | flops | bytes accessed | tf_op | source)
XLA Modules:
  0.0 19.1 jit_solution(9185065583946015518)
XLA Ops:
  0.6 17.7 %linker.1 = (f32[20,2,8,128]{3,2,1,0:T(8,128)S(1)}, f32[2,8,128]{2,1,0:T(8,128)S(1)}, f32[2,128]{1,0:T(2,128)S(1)}) custom-call(f32[20,2,8,128]{3,2,1,0:T(8,128)} %slc_hbm.1, s32[8,128]{1,0:T(8,128)} %land_hbm.1), custom_call_target="tpu_custom_call" | custom-call | tf_op jit(solution)/shard_map/linker/pallas_call | solution.py:816
  18.4 0.7 %closing.1 = (f32[20,2,8,128]{3,2,1,0:T(8,128)}, f32[2,8,128]{2,1,0:T(8,128)}, f32[2]{0:T(128)}) custom-call(f32[20,2,8,128]{3,2,1,0:T(8,128)S(1)} %get-tuple-element.6.linked_in, f32[2,8,128]{2,1,0:T(8,128)S(1)} %get-tuple-element.7.comp_in, f32[2,128]{1,0:T(2,128)S(1)} %get-tuple-element.8.total), custom_call_target="tpu_custom_call" | custom-call | tf_op jit(solution)/shard_map/closing/pallas_call | solution.py:860

commit v5 on v4

--- a/solution.py
+++ b/solution.py
@@ -26,7 +26,7 @@
 def pair_groups():
     groups = [[(s, (s + lag) % SUB) for s in range(SUB)] for lag in range(SUB // 2)]
     half = SUB // 2
-    groups.append([(s, s + half) for s in range(half)] + [(M - 2, M - 1), (M - 2, M - 2), (M - 1, M - 1)])
+    groups.insert(1, [(s, s + half) for s in range(half)] + [(M - 2, M - 1), (M - 2, M - 2), (M - 1, M - 1)])
     groups.append([(s, M - 2) for s in range(SUB)])
     groups.append([(s, M - 1) for s in range(SUB)])
     return groups
@@ -342,9 +342,9 @@
         lead = [tile(c, 0) for c in range(2)]
         if unit == 0:
             return lead, lead
-        if unit < SUB // 2:
-            return lead, [pltpu.roll(v, SUB - unit, 0) for v in lead]
-        if unit == SUB // 2:
+        if 1 < unit <= SUB // 2:
+            return lead, [pltpu.roll(v, SUB + 1 - unit, 0) for v in lead]
+        if unit == 1:
             left, right = [], []
             for c in range(2):
                 mid, late = tile(c, SUB // 2), tile(c, SUB - M + 5)
@@ -555,12 +555,10 @@
                 squares = [x * x + y * y for x, y in zip(re, im)]
                 while len(squares) > 1:
                     squares = [sum(squares[k + 1 : k + 2], squares[k]) for k in range(0, len(squares), 2)]
-                length = jnp.sqrt(squares[0])
-                if gain is not None:
-                    length = length * gain
-                inverse = 1.0 / jnp.maximum(length, 1.0)
+                square = squares[0] if gain is None else squares[0] * (gain * gain)
+                inverse = lax.rsqrt(jnp.maximum(square, 1.0))
                 gain = inverse if gain is None else gain * inverse
-            return length, gain, re, im
+            return jnp.sqrt(square), gain, re, im
 
     def finish(m, number, length, gain, re, im):
         comp_re = comp_im = None
@@ -794,8 +792,9 @@
     ]
     for copy in copies[:2]:
         copy.start()
+    sums = jnp.sum(total[...], axis=1, keepdims=True) * (1.0 / pixels)
     for m in range(MS):
-        scalars[m] = jnp.sum(total[m : m + 1]) / pixels
+        scalars[m] = sums[m, 0]
     copies[2].start()
     for copy in copies:
         copy.wait()

time: 19.3 us -> 19.3 us (level)
  no operation moved by 1% of the time
where the time goes in v5:
time: 19.3 us; the launch traced here: 19.1 us
  Pallas kernels  18.4 us (95%)
  between operations  0.64 us (3%)
    pallas_call x1, Pallas kernels, shards(): pl.pallas_call(functools.partial(kernel, row_count, col_count, direct), o...  17.7 us
    pallas_call x1, Pallas kernels, shards(): pl.pallas_call(functools.partial(closing, rows * cols * devices), out_sha...  0.71 us

profile of v5, /device:TPU:0, one launch (start us, length us, event | category | flops | bytes accessed | tf_op | source)
XLA Modules:
  0.0 19.1 jit_solution(17394529995944022092)
XLA Ops:
  0.6 17.7 %linker.1 = (f32[20,2,8,128]{3,2,1,0:T(8,128)S(1)}, f32[2,8,128]{2,1,0:T(8,128)S(1)}, f32[2,128]{1,0:T(2,128)S(1)}) custom-call(f32[20,2,8,128]{3,2,1,0:T(8,128)} %slc_hbm.1, s32[8,128]{1,0:T(8,128)} %land_hbm.1), custom_call_target="tpu_custom_call" | custom-call | tf_op jit(solution)/shard_map/linker/pallas_call | solution.py:815
  18.4 0.7 %closing.1 = (f32[20,2,8,128]{3,2,1,0:T(8,128)}, f32[2,8,128]{2,1,0:T(8,128)}, f32[2]{0:T(128)}) custom-call(f32[20,2,8,128]{3,2,1,0:T(8,128)S(1)} %get-tuple-element.6.linked_in, f32[2,8,128]{2,1,0:T(8,128)S(1)} %get-tuple-element.7.comp_in, f32[2,128]{1,0:T(2,128)S(1)} %get-tuple-element.8.total), custom_call_target="tpu_custom_call" | custom-call | tf_op jit(solution)/shard_map/closing/pallas_call | solution.py:859

commit v6 on v5

--- a/solution.py
+++ b/solution.py
@@ -163,8 +163,6 @@
     ] + [
         pltpu.make_async_copy(slc_hbm.at[pl.ds(m * M, M)], slc.at[pl.ds(m * M, M)], load_sem.at[m]) for m in range(MS)
     ]
-    for load in loads:
-        load.start()
 
     def existing(dr, dc, far=1):
         ok = None
@@ -197,6 +195,8 @@
 
     barrier = pltpu.get_barrier_semaphore()
     expected = greet(barrier, 1)
+    for load in loads:
+        load.start()
     offsets = waves(row_count, col_count)
     pending = []
 
@@ -406,11 +406,11 @@
             ybuf[unit, r * 2 * SUB : (r + 1) * 2 * SUB, 0:cols] = high
             ybuf[unit, r * 2 * SUB : (r + 1) * 2 * SUB, cols:] = low
 
-    def emit_main(unit, main, target, step):
+    def emit_main(unit, main, target, step, height=2 * SUB):
         for r in range(rows):
             at = r * step + unit * 2 * SUB
-            target[at : at + 2 * SUB, :] = (
-                main[r * 2 * SUB : (r + 1) * 2 * SUB, :] + ebuf[r, unit * 2 * SUB : (unit + 1) * 2 * SUB]
+            target[at : at + height, :] = (
+                main[r * 2 * SUB : r * 2 * SUB + height, :] + ebuf[r, unit * 2 * SUB : unit * 2 * SUB + height]
             )
 
     def both_halves(pair):
@@ -437,7 +437,7 @@
         for unit in range(len(GROUPS)):
             emit_lines(unit, [fresh_values(m, e, unit) for e in far_lines])
             main = jnp.dot(ybuf[unit], w_main[...], preferred_element_type=jnp.float32)
-            emit_main(unit, main, zbuf, FRESH_STEP)
+            emit_main(unit, main, zbuf, FRESH_STEP, 2 * SUB if unit else SUB)
 
     def comp_row(e, c):
         if e < REACH:

time: 19.3 us -> 19.2 us (level)
  no operation moved by 1% of the time
where the time goes in v6:
time: 19.2 us; the launch traced here: 19.1 us
  Pallas kernels  18.4 us (96%)
  between operations  0.64 us (3%)
    pallas_call x1, Pallas kernels, shards(): pl.pallas_call(functools.partial(kernel, row_count, col_count, direct), o...  17.7 us
    pallas_call x1, Pallas kernels, shards(): pl.pallas_call(functools.partial(closing, rows * cols * devices), out_sha...  0.71 us

profile of v6, /device:TPU:0, one launch (start us, length us, event | category | flops | bytes accessed | tf_op | source)
XLA Modules:
  0.0 19.1 jit_solution(3226678571599144852)
XLA Ops:
  0.6 17.7 %linker.1 = (f32[20,2,8,128]{3,2,1,0:T(8,128)S(1)}, f32[2,8,128]{2,1,0:T(8,128)S(1)}, f32[2,128]{1,0:T(2,128)S(1)}) custom-call(f32[20,2,8,128]{3,2,1,0:T(8,128)} %slc_hbm.1, s32[8,128]{1,0:T(8,128)} %land_hbm.1), custom_call_target="tpu_custom_call" | custom-call | tf_op jit(solution)/shard_map/linker/pallas_call | solution.py:815
  18.4 0.7 %closing.1 = (f32[20,2,8,128]{3,2,1,0:T(8,128)}, f32[2,8,128]{2,1,0:T(8,128)}, f32[2]{0:T(128)}) custom-call(f32[20,2,8,128]{3,2,1,0:T(8,128)S(1)} %get-tuple-element.6.linked_in, f32[2,8,128]{2,1,0:T(8,128)S(1)} %get-tuple-element.7.comp_in, f32[2,128]{1,0:T(2,128)S(1)} %get-tuple-element.8.total), custom_call_target="tpu_custom_call" | custom-call | tf_op jit(solution)/shard_map/closing/pallas_call | solution.py:859
